TPU v7x, 256 devices: a whole 4x4x8 slice. The times are simulated.
256 devices in a mesh: samp: 32 (over y, z_hi, x), tile: 8 (over z_lo, core).
Axes of the slice: x: 4, y: 4, z: 8 (z_hi: 2, z_lo: 4; z = z_hi * 4 + z_lo), core: 2. Of those that a mesh axis runs over, the one named last changes fastest.
Arguments:
- traits: bfloat16 [32768, 1024], P('samp'), may hold values from -300 to 300
- covariates: bfloat16 [32768, 32], P('samp'), may hold values from -6 to 6
- genotypes: int32 [32768, 2048], P('samp', 'tile'), may hold values from 0 to 2
- shuffles: int32 [6, 32768], P(None, 'samp'), may hold values from 0 to 32767, as said below
Outputs:
- observed: float32 [1024, 2048], P('samp', 'tile')
- perm_max: float32 [6, 1024], P(None, 'samp')
Inputs may be any that keep to these rules, and one draw needn't show every extreme that they name: Row p of shuffles maps each aligned block of 1024 samples one to one onto the same block's samples.
All inputs are finite; a program needn't handle non-finite values.
Results may differ from a plain program's by a relative error of at most 0.0045.
Values sent between devices are 32-bit elements; how exact they have to be, the bound alone decides.
A program may use at most 64 MiB of HBM per device.

v0:
```python
import math

import jax
import jax.numpy as jnp
from jax import lax
from jax.sharding import PartitionSpec as P

C = 32


epsilon = 1e-05


def filled_up(lines, count):
    spare = -len(lines) % count
    return jnp.pad(lines, [(0, spare)] + [(0, 0)] * (lines.ndim - 1))


def joined_along(blocks, dim):
    lengths = list(blocks.shape[1:])
    lengths[dim] *= blocks.shape[0]
    return jnp.moveaxis(blocks, 0, dim).reshape(lengths)


def copy_for_each(value, axis):
    copies = jnp.broadcast_to(value, (lax.axis_size(axis), *value.shape))
    return lax.all_to_all(copies, axis, split_axis=0, concat_axis=0, tiled=True)


def gathered_copies(value, axis, dim):
    return joined_along(copy_for_each(value, axis), dim)


def in_blocks(value, dim, count):
    lengths = value.shape
    blocks = value.reshape(*lengths[:dim], count, lengths[dim] // count, *lengths[dim + 1 :])
    return jnp.moveaxis(blocks, dim, 0)


def sum_at_owner(value, axis, dim):
    count = lax.axis_size(axis)
    blocks = lax.all_to_all(in_blocks(value, dim, count), axis, 0, 0, tiled=True)
    return jnp.sum(blocks, axis=0)


def total_of(value, axes):
    padded = filled_up(value, lax.axis_size(axes))
    whole = gathered_copies(sum_at_owner(padded, axes, 0), axes, 0)
    return lax.slice_in_dim(whole, 0, len(value)).reshape(value.shape)


def together(arrays, axis):
    line, at, outs = (jnp.concatenate([a.reshape(-1) for a in arrays]), 0, [])
    running = total_of(line, axis)
    for a in arrays:
        outs.append(running[at : at + a.size].reshape(a.shape))
        at += a.size
    return tuple(outs)


def over_copies(value, axis):
    everything = copy_for_each(value, axis)
    return jnp.sum(everything, axis=0)


def packed_total(arrays, axis):
    ends = [0]
    for a in arrays:
        ends.append(ends[-1] + a.size)
    running = over_copies(jnp.concatenate([a.ravel() for a in arrays]), axis)
    return tuple((running[b:e].reshape(a.shape) for a, b, e in zip(arrays, ends, ends[1:])))


def taken_together(value, axis):
    return copy_for_each(value, axis).max(axis=0)


def cholesky_solve(factor, rhs):
    first = lax.linalg.triangular_solve(factor, rhs, left_side=True, lower=True)
    return lax.linalg.triangular_solve(factor, first, left_side=True, lower=True, transpose_a=True)


def cross_local(left, right):
    return lax.dot_general(
        left, right, (((0,), (0,)), ((), ())), preferred_element_type=jnp.float32
    )


def shards(traits, covariates, genotypes, shuffles):
    groups = lax.axis_size("samp")
    own_index = lax.axis_index("samp")
    local_rows = traits.shape[0]
    samples = local_rows * groups
    share_rows = traits.shape[1] // groups
    ones = jnp.ones((local_rows, 1), jnp.bfloat16)
    design = jnp.concatenate([ones, covariates], axis=1)
    dosage = genotypes.astype(jnp.bfloat16)
    gram = cross_local(design, design)
    xty = cross_local(design, traits)
    xtg = cross_local(design, dosage)
    gram, xty, xtg = together((gram, xty, xtg), "samp")
    factor = jnp.linalg.cholesky(gram)
    coef_traits = cholesky_solve(factor, xty).astype(jnp.bfloat16)
    coef_geno = cholesky_solve(factor, xtg).astype(jnp.bfloat16)
    resid_traits = traits.astype(jnp.float32) - jnp.dot(
        design, coef_traits, preferred_element_type=jnp.float32
    )
    resid_geno = dosage.astype(jnp.float32) - jnp.dot(
        design, coef_geno, preferred_element_type=jnp.float32
    )
    sum_traits, sum_geno = packed_total(
        (jnp.sum(resid_traits * resid_traits, axis=0), jnp.sum(resid_geno * resid_geno, axis=0)),
        "samp",
    )
    mean_traits = sum_traits / samples
    mean_geno = sum_geno / samples
    rt_rows = resid_traits.astype(jnp.bfloat16)
    rg_rows = resid_geno.astype(jnp.bfloat16)
    scale_traits = lax.rsqrt(mean_traits + epsilon)
    scale_geno = lax.rsqrt(mean_geno + epsilon)
    factor_z = math.sqrt(samples - C - 2) / samples
    own_scale = lax.dynamic_slice_in_dim(scale_traits, own_index * share_rows, share_rows, 0)

    def owned_scores(trait_rows):
        owned = sum_at_owner(cross_local(trait_rows, rg_rows), "samp", 0)
        return owned * own_scale[:, None] * scale_geno[None, :] * factor_z

    observed = owned_scores(rt_rows)
    peaks = []
    for perm_id in range(shuffles.shape[0]):
        local_order = shuffles[perm_id] - own_index * local_rows
        shuffled = jnp.take(rt_rows, local_order, axis=0)
        peak = jnp.max(jnp.abs(owned_scores(shuffled)), axis=1)
        peaks.append(peak)
    perm_max = jnp.stack(peaks, axis=0)
    perm_max = taken_together(perm_max, "tile")
    return (observed, perm_max)


def solution(mesh):
    placed = (P("samp", None), P("samp", None), P("samp", "tile"), P(None, "samp"))
    return jax.shard_map(
        shards,
        mesh=mesh,
        in_specs=placed,
        out_specs=(P("samp", "tile"), P(None, "samp")),
        check_vma=False,
    )
```

profile of v0, /device:TPU:1, one launch (start us, length us, event | category | flops | bytes accessed | tf_op | source)
XLA Modules:
  0.0 306.3 jit_solution(18319217605577383872)
XLA Ops:
  5.4 14.5 %all-to-all-start = ((f32[32,1,1355]{2,1,0:T(1,128)}), f32[32,1,1355]{2,1,0:T(1,128)S(1)}, u32[]{:S(2)}, u32[]{:S(2)}) async-start(f32[32,1,1355]{2,1,0:T(1,128)} %all_to_all.38), calls=%async_computation | async-start | bytes 360448 | tf_op jit(solution)/shard_map/all_to_all | solution.py:42
  19.9 11.7 %all-to-all-done = f32[32,1,1355]{2,1,0:T(1,128)S(1)} async-done(((f32[32,1,1355]{2,1,0:T(1,128)}), f32[32,1,1355]{2,1,0:T(1,128)S(1)}, u32[]{:S(2)}, u32[]{:S(2)}) %all-to-all-start) | async-done | bytes 173472 | tf_op jit(solution)/shard_map/all_to_all | solution.py:42
  32.5 3.9 %all-to-all-start.1 = ((f32[32,1,1355]{2,1,0:T(1,128)}), f32[32,1,1355]{2,1,0:T(1,128)S(1)}, u32[]{:S(2)}, u32[]{:S(2)}) async-start(f32[32,1,1355]{2,1,0:T(1,128)} %broadcast_in_dim.17), calls=%async_computation.1 | async-start | bytes 360448 | tf_op jit(solution)/shard_map/all_to_all | solution.py:27
  36.4 11.6 %all-to-all-done.1 = f32[32,1,1355]{2,1,0:T(1,128)S(1)} async-done(((f32[32,1,1355]{2,1,0:T(1,128)}), f32[32,1,1355]{2,1,0:T(1,128)S(1)}, u32[]{:S(2)}, u32[]{:S(2)}) %all-to-all-start.1) | async-done | bytes 173472 | tf_op jit(solution)/shard_map/all_to_all | solution.py:27
  60.6 3.9 %all-to-all-start.3 = ((f32[32,1,1280]{2,1,0:T(1,128)}), f32[32,1,1280]{2,1,0:T(1,128)S(1)}, u32[]{:S(2)}, u32[]{:S(2)}) async-start(f32[32,1,1280]{2,1,0:T(1,128)} %broadcast_in_dim.18), calls=%async_computation.3 | async-start | bytes 327680 | tf_op jit(solution)/shard_map/all_to_all | solution.py:27
  64.5 5.4 %gather_fusion.5 = bf16[1024,1024]{1,0:T(8,128)(2,1)} fusion(bf16[1024,1024]{1,0:T(8,128)(2,1)S(1)} %get-tuple-element.10, s32[1024]{0:T(1024)S(1)} %fusion.50), kind=kCustom, calls=%fused_computation.5.clone | custom fusion | bytes 4198400 | tf_op jit(solution)/shard_map/jit(_take)/gather | solution.py:132
  69.8 3.5 %fusion.1 = f32[1024,256]{1,0:T(8,128)} fusion(bf16[1024,256]{1,0:T(8,128)(2,1)S(1)} %get-tuple-element.12, bf16[1024,1024]{1,0:T(8,128)(2,1)} %gather_fusion.5, pred[1024]{0:T(1024)(128)(4,1)S(1)} %compare_and_fusion), kind=kOutput, calls=%fused_computation.9 | convolution fusion | flops 537919488 | bytes 3671040 | tf_op jit(solution)/shard_map/dot_general | solution.py:84
  76.0 9.0 %all-to-all-start.9 = ((f32[32,32,256]{2,1,0:T(8,128)}), f32[32,32,256]{2,1,0:T(8,128)S(1)}, u32[]{:S(2)}, u32[]{:S(2)}) async-start(f32[32,32,256]{2,1,0:T(8,128)} %bitcast.51), calls=%async_computation.9 | async-start | bytes 2097152 | tf_op jit(solution)/shard_map/all_to_all | solution.py:42
  85.0 5.4 %gather_fusion = bf16[1024,1024]{1,0:T(8,128)(2,1)} fusion(bf16[1024,1024]{1,0:T(8,128)(2,1)S(1)} %get-tuple-element.10, s32[1024]{0:T(1024)S(1)} %fusion.45), kind=kCustom, calls=%fused_computation.clone | custom fusion | bytes 4198400 | tf_op jit(solution)/shard_map/jit(_take)/gather | solution.py:132
  90.4 3.6 %fusion.11 = f32[1024,256]{1,0:T(8,128)} fusion(bf16[1024,256]{1,0:T(8,128)(2,1)} %copy-done.2, bf16[1024,1024]{1,0:T(8,128)(2,1)} %gather_fusion, pred[1024]{0:T(1024)(128)(4,1)S(1)} %compare_and_fusion.5), kind=kOutput, calls=%fused_computation.19 | convolution fusion | flops 537919488 | bytes 3671040 | tf_op jit(solution)/shard_map/dot_general | solution.py:84
  94.0 9.1 %all-to-all-done.9 = f32[32,32,256]{2,1,0:T(8,128)S(1)} async-done(((f32[32,32,256]{2,1,0:T(8,128)}), f32[32,32,256]{2,1,0:T(8,128)S(1)}, u32[]{:S(2)}, u32[]{:S(2)}) %all-to-all-start.9) | async-done | bytes 1048608 | tf_op jit(solution)/shard_map/all_to_all | solution.py:42
  103.1 4.7 %all-to-all-start.4 = ((f32[32,32,256]{2,1,0:T(8,128)}), f32[32,32,256]{2,1,0:T(8,128)}, u32[]{:S(2)}, u32[]{:S(2)}) async-start(f32[32,32,256]{2,1,0:T(8,128)} %bitcast.52), calls=%async_computation.4 | async-start | bytes 2097152 | tf_op jit(solution)/shard_map/all_to_all | solution.py:42
  107.8 5.4 %gather_fusion.1 = bf16[1024,1024]{1,0:T(8,128)(2,1)} fusion(bf16[1024,1024]{1,0:T(8,128)(2,1)S(1)} %get-tuple-element.10, s32[1024]{0:T(1024)S(1)} %fusion.46), kind=kCustom, calls=%fused_computation.1.clone | custom fusion | bytes 4198400 | tf_op jit(solution)/shard_map/jit(_take)/gather | solution.py:132
  113.1 3.6 %fusion.9 = f32[1024,256]{1,0:T(8,128)} fusion(bf16[1024,256]{1,0:T(8,128)(2,1)} %copy-done.2, bf16[1024,1024]{1,0:T(8,128)(2,1)} %gather_fusion.1, pred[1024]{0:T(1024)(128)(4,1)S(1)} %compare_and_fusion.4), kind=kOutput, calls=%fused_computation.17 | convolution fusion | flops 537919488 | bytes 3671040 | tf_op jit(solution)/shard_map/dot_general | solution.py:84
  116.7 5.9 %all-to-all-done.4 = f32[32,32,256]{2,1,0:T(8,128)} async-done(((f32[32,32,256]{2,1,0:T(8,128)}), f32[32,32,256]{2,1,0:T(8,128)}, u32[]{:S(2)}, u32[]{:S(2)}) %all-to-all-start.4) | async-done | bytes 1048608 | tf_op jit(solution)/shard_map/all_to_all | solution.py:42
  122.6 8.4 %all-to-all-start.5 = ((f32[32,32,256]{2,1,0:T(8,128)}), f32[32,32,256]{2,1,0:T(8,128)}, u32[]{:S(2)}, u32[]{:S(2)}) async-start(f32[32,32,256]{2,1,0:T(8,128)} %bitcast.53), calls=%async_computation.5 | async-start | bytes 2097152 | tf_op jit(solution)/shard_map/all_to_all | solution.py:42
  131.0 5.4 %gather_fusion.2 = bf16[1024,1024]{1,0:T(8,128)(2,1)} fusion(bf16[1024,1024]{1,0:T(8,128)(2,1)S(1)} %get-tuple-element.10, s32[1024]{0:T(1024)S(1)} %fusion.47), kind=kCustom, calls=%fused_computation.2.clone | custom fusion | bytes 4198400 | tf_op jit(solution)/shard_map/jit(_take)/gather | solution.py:132
  136.4 3.6 %fusion.7 = f32[1024,256]{1,0:T(8,128)} fusion(bf16[1024,256]{1,0:T(8,128)(2,1)} %copy-done.2, bf16[1024,1024]{1,0:T(8,128)(2,1)} %gather_fusion.2, pred[1024]{0:T(1024)(128)(4,1)S(1)} %compare_and_fusion.3), kind=kOutput, calls=%fused_computation.15 | convolution fusion | flops 537919488 | bytes 3671040 | tf_op jit(solution)/shard_map/dot_general | solution.py:84
  140.0 10.4 %all-to-all-done.5 = f32[32,32,256]{2,1,0:T(8,128)} async-done(((f32[32,32,256]{2,1,0:T(8,128)}), f32[32,32,256]{2,1,0:T(8,128)}, u32[]{:S(2)}, u32[]{:S(2)}) %all-to-all-start.5) | async-done | bytes 1048608 | tf_op jit(solution)/shard_map/all_to_all | solution.py:42
  150.5 9.2 %all-to-all-start.6 = ((f32[32,32,256]{2,1,0:T(8,128)}), f32[32,32,256]{2,1,0:T(8,128)}, u32[]{:S(2)}, u32[]{:S(2)}) async-start(f32[32,32,256]{2,1,0:T(8,128)} %bitcast.54), calls=%async_computation.6 | async-start | bytes 2097152 | tf_op jit(solution)/shard_map/all_to_all | solution.py:42
  159.7 5.4 %gather_fusion.3 = bf16[1024,1024]{1,0:T(8,128)(2,1)} fusion(bf16[1024,1024]{1,0:T(8,128)(2,1)S(1)} %get-tuple-element.10, s32[1024]{0:T(1024)S(1)} %fusion.48), kind=kCustom, calls=%fused_computation.3.clone | custom fusion | bytes 4198400 | tf_op jit(solution)/shard_map/jit(_take)/gather | solution.py:132
  165.1 3.6 %fusion.5 = f32[1024,256]{1,0:T(8,128)} fusion(bf16[1024,256]{1,0:T(8,128)(2,1)} %copy-done.2, bf16[1024,1024]{1,0:T(8,128)(2,1)} %gather_fusion.3, pred[1024]{0:T(1024)(128)(4,1)S(1)} %compare_and_fusion.2), kind=kOutput, calls=%fused_computation.13 | convolution fusion | flops 537919488 | bytes 3671040 | tf_op jit(solution)/shard_map/dot_general | solution.py:84
  168.7 11.7 %all-to-all-done.6 = f32[32,32,256]{2,1,0:T(8,128)} async-done(((f32[32,32,256]{2,1,0:T(8,128)}), f32[32,32,256]{2,1,0:T(8,128)}, u32[]{:S(2)}, u32[]{:S(2)}) %all-to-all-start.6) | async-done | bytes 1048608 | tf_op jit(solution)/shard_map/all_to_all | solution.py:42
  180.5 9.3 %all-to-all-start.7 = ((f32[32,32,256]{2,1,0:T(8,128)}), f32[32,32,256]{2,1,0:T(8,128)}, u32[]{:S(2)}, u32[]{:S(2)}) async-start(f32[32,32,256]{2,1,0:T(8,128)} %bitcast.50), calls=%async_computation.7 | async-start | bytes 2097152 | tf_op jit(solution)/shard_map/all_to_all | solution.py:42
  189.8 5.4 %gather_fusion.4 = bf16[1024,1024]{1,0:T(8,128)(2,1)} fusion(bf16[1024,1024]{1,0:T(8,128)(2,1)S(1)} %get-tuple-element.10, s32[1024]{0:T(1024)S(1)} %fusion.49), kind=kCustom, calls=%fused_computation.4.clone | custom fusion | bytes 4198400 | tf_op jit(solution)/shard_map/jit(_take)/gather | solution.py:132
  195.1 3.6 %fusion.3 = f32[1024,256]{1,0:T(8,128)} fusion(bf16[1024,256]{1,0:T(8,128)(2,1)} %copy-done.2, bf16[1024,1024]{1,0:T(8,128)(2,1)} %gather_fusion.4, pred[1024]{0:T(1024)(128)(4,1)S(1)} %compare_and_fusion.1), kind=kOutput, calls=%fused_computation.11 | convolution fusion | flops 537919488 | bytes 3671040 | tf_op jit(solution)/shard_map/dot_general | solution.py:84
  198.7 12.1 %all-to-all-done.7 = f32[32,32,256]{2,1,0:T(8,128)} async-done(((f32[32,32,256]{2,1,0:T(8,128)}), f32[32,32,256]{2,1,0:T(8,128)}, u32[]{:S(2)}, u32[]{:S(2)}) %all-to-all-start.7) | async-done | bytes 1048608 | tf_op jit(solution)/shard_map/all_to_all | solution.py:42
  210.8 8.7 %all-to-all-start.8 = ((f32[32,32,256]{2,1,0:T(8,128)}), f32[32,32,256]{2,1,0:T(8,128)}, u32[]{:S(2)}, u32[]{:S(2)}) async-start(f32[32,32,256]{2,1,0:T(8,128)} %bitcast.55), calls=%async_computation.8 | async-start | bytes 2097152 | tf_op jit(solution)/shard_map/all_to_all | solution.py:42
  222.3 18.2 %all-to-all-done.8 = f32[32,32,256]{2,1,0:T(8,128)} async-done(((f32[32,32,256]{2,1,0:T(8,128)}), f32[32,32,256]{2,1,0:T(8,128)}, u32[]{:S(2)}, u32[]{:S(2)}) %all-to-all-start.8) | async-done | bytes 1048608 | tf_op jit(solution)/shard_map/all_to_all | solution.py:42
  240.5 8.8 %all-to-all-start.2 = ((f32[32,32,256]{2,1,0:T(8,128)}), f32[32,32,256]{2,1,0:T(8,128)S(1)}, u32[]{:S(2)}, u32[]{:S(2)}) async-start(f32[32,32,256]{2,1,0:T(8,128)} %bitcast.49), calls=%async_computation.2 | async-start | bytes 2097152 | tf_op jit(solution)/shard_map/all_to_all | solution.py:42
  256.1 14.3 %all-to-all-done.2 = f32[32,32,256]{2,1,0:T(8,128)S(1)} async-done(((f32[32,32,256]{2,1,0:T(8,128)}), f32[32,32,256]{2,1,0:T(8,128)S(1)}, u32[]{:S(2)}, u32[]{:S(2)}) %all-to-all-start.2) | async-done | bytes 1048608 | tf_op jit(solution)/shard_map/all_to_all | solution.py:42
  271.4 33.0 %all_to_all.61 = f32[8,1,192]{2,1,0:T(1,128)S(1)} all-to-all(f32[8,1,192]{2,1,0:T(1,128)S(1)} %reshape.174), channel_id=1, replica_groups=mesh['samp'=32,'tile'=8] {'tile'}, dimensions={0} | all-to-all | bytes 12288 | tf_op jit(solution)/shard_map/all_to_all | solution.py:27
  (76 shorter events, 33.3 us)
Async XLA Ops:
  0.6 3.4 %copy-start.1 = (bf16[1024,32]{0,1:T(8,128)(2,1)S(1)}, bf16[1024,32]{0,1:T(8,128)(2,1)}, u32[]{:S(2)}) copy-start(bf16[1024,32]{0,1:T(8,128)(2,1)} %param.7) | copy-start | bytes 196612
  0.6 3.4 %copy-start = (s32[1024,256]{1,0:T(8,128)S(1)}, s32[1024,256]{1,0:T(8,128)}, u32[]{:S(2)}) copy-start(s32[1024,256]{1,0:T(8,128)} %param.8) | copy-start | bytes 3145732
  1.9 18.0 %copy-start.3 = (s32[6,1024]{1,0:T(8,128)S(1)}, s32[6,1024]{1,0:T(8,128)}, u32[]{:S(2)}) copy-start(s32[6,1024]{1,0:T(8,128)} %param.9) | copy-start | bytes 73732
  5.4 26.2 %all-to-all-start = ((f32[32,1,1355]{2,1,0:T(1,128)}), f32[32,1,1355]{2,1,0:T(1,128)S(1)}, u32[]{:S(2)}, u32[]{:S(2)}) async-start(f32[32,1,1355]{2,1,0:T(1,128)} %all_to_all.38), calls=%async_computation | async-start | bytes 360448 | tf_op jit(solution)/shard_map/all_to_all | solution.py:42
  32.5 15.5 %all-to-all-start.1 = ((f32[32,1,1355]{2,1,0:T(1,128)}), f32[32,1,1355]{2,1,0:T(1,128)S(1)}, u32[]{:S(2)}, u32[]{:S(2)}) async-start(f32[32,1,1355]{2,1,0:T(1,128)} %broadcast_in_dim.17), calls=%async_computation.1 | async-start | bytes 360448 | tf_op jit(solution)/shard_map/all_to_all | solution.py:27
  56.7 13.1 %copy-start.2 = (bf16[1024,256]{1,0:T(8,128)(2,1)}, bf16[1024,256]{1,0:T(8,128)(2,1)S(1)}, u32[]{:S(2)}) copy-start(bf16[1024,256]{1,0:T(8,128)(2,1)S(1)} %get-tuple-element.12) | copy-start | bytes 1572868
  60.6 15.4 %all-to-all-start.3 = ((f32[32,1,1280]{2,1,0:T(1,128)}), f32[32,1,1280]{2,1,0:T(1,128)S(1)}, u32[]{:S(2)}, u32[]{:S(2)}) async-start(f32[32,1,1280]{2,1,0:T(1,128)} %broadcast_in_dim.18), calls=%async_computation.3 | async-start | bytes 327680 | tf_op jit(solution)/shard_map/all_to_all | solution.py:27
  76.0 27.1 %all-to-all-start.9 = ((f32[32,32,256]{2,1,0:T(8,128)}), f32[32,32,256]{2,1,0:T(8,128)S(1)}, u32[]{:S(2)}, u32[]{:S(2)}) async-start(f32[32,32,256]{2,1,0:T(8,128)} %bitcast.51), calls=%async_computation.9 | async-start | bytes 2097152 | tf_op jit(solution)/shard_map/all_to_all | solution.py:42
  103.1 19.5 %all-to-all-start.4 = ((f32[32,32,256]{2,1,0:T(8,128)}), f32[32,32,256]{2,1,0:T(8,128)}, u32[]{:S(2)}, u32[]{:S(2)}) async-start(f32[32,32,256]{2,1,0:T(8,128)} %bitcast.52), calls=%async_computation.4 | async-start | bytes 2097152 | tf_op jit(solution)/shard_map/all_to_all | solution.py:42
  122.6 27.9 %all-to-all-start.5 = ((f32[32,32,256]{2,1,0:T(8,128)}), f32[32,32,256]{2,1,0:T(8,128)}, u32[]{:S(2)}, u32[]{:S(2)}) async-start(f32[32,32,256]{2,1,0:T(8,128)} %bitcast.53), calls=%async_computation.5 | async-start | bytes 2097152 | tf_op jit(solution)/shard_map/all_to_all | solution.py:42
  150.5 30.0 %all-to-all-start.6 = ((f32[32,32,256]{2,1,0:T(8,128)}), f32[32,32,256]{2,1,0:T(8,128)}, u32[]{:S(2)}, u32[]{:S(2)}) async-start(f32[32,32,256]{2,1,0:T(8,128)} %bitcast.54), calls=%async_computation.6 | async-start | bytes 2097152 | tf_op jit(solution)/shard_map/all_to_all | solution.py:42
  180.5 30.4 %all-to-all-start.7 = ((f32[32,32,256]{2,1,0:T(8,128)}), f32[32,32,256]{2,1,0:T(8,128)}, u32[]{:S(2)}, u32[]{:S(2)}) async-start(f32[32,32,256]{2,1,0:T(8,128)} %bitcast.50), calls=%async_computation.7 | async-start | bytes 2097152 | tf_op jit(solution)/shard_map/all_to_all | solution.py:42
  210.8 29.7 %all-to-all-start.8 = ((f32[32,32,256]{2,1,0:T(8,128)}), f32[32,32,256]{2,1,0:T(8,128)}, u32[]{:S(2)}, u32[]{:S(2)}) async-start(f32[32,32,256]{2,1,0:T(8,128)} %bitcast.55), calls=%async_computation.8 | async-start | bytes 2097152 | tf_op jit(solution)/shard_map/all_to_all | solution.py:42
  240.5 29.8 %all-to-all-start.2 = ((f32[32,32,256]{2,1,0:T(8,128)}), f32[32,32,256]{2,1,0:T(8,128)S(1)}, u32[]{:S(2)}, u32[]{:S(2)}) async-start(f32[32,32,256]{2,1,0:T(8,128)} %bitcast.49), calls=%async_computation.2 | async-start | bytes 2097152 | tf_op jit(solution)/shard_map/all_to_all | solution.py:42
where the time goes:
time: 308 us; the launch traced here: 306 us
  waiting for transfers between devices  108 us (35%)
  starting transfers between devices  80.2 us (26%)
  local copies, waits for them, and re-layouts  36.3 us (12%)
  blocking collectives  33 us (11%)
  matrix products  31.8 us (10%)
  other arithmetic  16.4 us (5%)
    all_to_all x8, waiting for transfers between devices, sum_at_owner(): lax.all_to_all(in_blocks(value, dim, count), axis, 0, 0, tiled=True)  93.4 us
    all_to_all x8, starting transfers between devices, sum_at_owner(): lax.all_to_all(in_blocks(value, dim, count), axis, 0, 0, tiled=True)  72.4 us
    all_to_all x1, blocking collectives, copy_for_each(): return lax.all_to_all(copies, axis, split_axis=0, concat_axis=0, tiled=True)  33 us
    gather x6, local copies, waits for them, and re-layouts, shards(): shuffled = jnp.take(rt_rows, local_order, axis=0)  32.2 us
    dot_general x10, matrix products, cross_local(): lax.dot_general(left, right, (((0,), (0,)), ((), ())), preferred_element_...  27.9 us
    all_to_all x2, waiting for transfers between devices, copy_for_each(): return lax.all_to_all(copies, axis, split_axis=0, concat_axis=0, tiled=True)  14.3 us
    all_to_all x2, starting transfers between devices, copy_for_each(): return lax.all_to_all(copies, axis, split_axis=0, concat_axis=0, tiled=True)  7.73 us
    reduce_sum x8, other arithmetic, sum_at_owner(): return jnp.sum(blocks, axis=0)  6.75 us
  transfers between devices with their start and end apart: 10, of which 10 were waited for; matrix products, arithmetic and copies ran while one was open for 21% of the time, Pallas kernels for 0%

commit v1 on v0

--- a/solution.py
+++ b/solution.py
@@ -1,14 +1,18 @@
+import functools
 import math
 
 import jax
 import jax.numpy as jnp
 from jax import lax
+from jax.experimental import pallas as pl
+from jax.experimental.pallas import tpu as pltpu
 from jax.sharding import PartitionSpec as P
 
 C = 32
 
 
 epsilon = 1e-05
+MESH = pl.DeviceIdType.MESH
 
 
 def filled_up(lines, count):
@@ -71,10 +75,6 @@
     return tuple((running[b:e].reshape(a.shape) for a, b, e in zip(arrays, ends, ends[1:])))
 
 
-def taken_together(value, axis):
-    return copy_for_each(value, axis).max(axis=0)
-
-
 def cholesky_solve(factor, rhs):
     first = lax.linalg.triangular_solve(factor, rhs, left_side=True, lower=True)
     return lax.linalg.triangular_solve(factor, first, left_side=True, lower=True, transpose_a=True)
@@ -84,6 +84,251 @@
     return lax.dot_general(
         left, right, (((0,), (0,)), ((), ())), preferred_element_type=jnp.float32
     )
+
+
+def scan_kernel(
+    yt_ref, g_ref, order_ref, st_ref, sg_ref, obs_ref, peak_ref,
+    q_ref, part, in1, mid, in2, low, inz, pm, pmin,
+    send1, recv1, send2, recv2, sendz, recvz, sendt, recvt,
+):
+    perms = order_ref.shape[0]
+    mats = perms + 1
+    s = lax.axis_index("samp")
+    t = lax.axis_index("tile")
+    x = lax.rem(s, 4)
+    zh = lax.rem(s // 4, 2)
+    y = s // 8
+    base = s * yt_ref.shape[1]
+
+    def at_x(v):
+        return s - x + lax.rem(v, 4)
+
+    def at_y(v):
+        return lax.rem(v, 4) * 8 + lax.rem(s, 8)
+
+    z_peer = s + 4 - 8 * zh
+    place = (x, y)
+    peers = ((at_x(x + 1), at_x(x + 3)), (at_y(y + 1), at_y(y + 3)))
+
+    barrier = pltpu.get_barrier_semaphore()
+    for peer in (*peers[0], *peers[1], z_peer):
+        pl.semaphore_signal(barrier, inc=1, device_id={"samp": peer}, device_id_type=MESH)
+    for d in range(1, 8):
+        pl.semaphore_signal(
+            barrier, inc=1, device_id={"tile": lax.rem(t + d, 8)}, device_id_type=MESH
+        )
+    pl.semaphore_wait(barrier, 12)
+
+    def remote(src, dst, send, recv, peer):
+        return pltpu.make_async_remote_copy(
+            src_ref=src, dst_ref=dst, send_sem=send, recv_sem=recv,
+            device_id={"samp": peer}, device_id_type=MESH,
+        )
+
+    def first_copy(h, m, k):
+        c = place[h]
+        blk = lax.rem(c + (2, 1, 2, 3, 1, 3)[k], 4)
+        uv = (0, 1, 1, 0, 0, 1)[k]
+        src = part.at[h, m, blk, uv]
+        if k >= 4:
+            src = in1.at[h, m, 0 if k == 4 else 2]
+        return remote(
+            src, in1.at[h, m, k], send1.at[h, m, k], recv1.at[h, m, k],
+            peers[h][(0, 0, 1, 1, 0, 1)[k]],
+        )
+
+    def second_copy(h, m, k):
+        c = place[1 - h]
+        blk = lax.rem(c + (2, 1, 2, 3, 1, 3)[k], 4)
+        uv = (0, 1, 1, 0, 0, 1)[k]
+        src = mid.at[h, m, blk, uv]
+        if k >= 4:
+            src = in2.at[h, m, 0 if k == 4 else 2]
+        return remote(
+            src, in2.at[h, m, k], send2.at[h, m, k], recv2.at[h, m, k],
+            peers[1 - h][(0, 0, 1, 1, 0, 1)[k]],
+        )
+
+    def z_copy(h, m):
+        return remote(
+            low.at[h, m, 1 - zh], inz.at[h, m], sendz.at[h, m], recvz.at[h, m], z_peer
+        )
+
+    def compute(m, rows_ref):
+        def block(yb, carry):
+            lines = yt_ref[pl.ds(pl.multiple_of(yb * 256, 256), 256), :]
+            out = jnp.dot(lines, rows_ref[...], preferred_element_type=jnp.float32)
+            for z in range(2):
+                for xb in range(4):
+                    at = (z * 4 + xb) * 32
+                    part[0, m, xb, z, yb] = out[at : at + 32, :128]
+                    part[1, m, yb, z, xb] = out[at : at + 32, 128:]
+            return carry
+
+        lax.fori_loop(0, 4, block, 0)
+
+    def permute(m):
+        order = order_ref[pl.ds(m - 1, 1), :] - base
+
+        def block(jb, carry):
+            target = lax.broadcasted_iota(jnp.int32, (256, order.shape[1]), 0) + jb * 256
+            hot = jnp.where(target == order, 1.0, 0.0).astype(jnp.bfloat16)
+            rows = jnp.dot(hot, g_ref[...], preferred_element_type=jnp.float32)
+            q_ref[pl.ds(pl.multiple_of(jb * 256, 256), 256), :] = rows.astype(jnp.bfloat16)
+            return carry
+
+        lax.fori_loop(0, 4, block, 0)
+
+    def stage1(m):
+        for k in (0, 2, 1, 3):
+            for h in range(2):
+                first_copy(h, m, k).start()
+
+    def stage2(m):
+        for h in range(2):
+            c = place[h]
+            first_copy(h, m, 0).wait_recv()
+            in1[h, m, 0] = in1[h, m, 0] + part[h, m, lax.rem(c + 1, 4), 0]
+            first_copy(h, m, 4).start()
+            first_copy(h, m, 2).wait_recv()
+            in1[h, m, 2] = in1[h, m, 2] + part[h, m, lax.rem(c + 3, 4), 1]
+            first_copy(h, m, 5).start()
+
+    def stage3(m):
+        for h in range(2):
+            c = place[h]
+            for k in (1, 3, 4, 5):
+                first_copy(h, m, k).wait_recv()
+            mid[h, m, :, 0] = part[h, m, c, 0] + in1[h, m, 3] + in1[h, m, 4]
+            mid[h, m, :, 1] = part[h, m, c, 1] + in1[h, m, 1] + in1[h, m, 5]
+            for k in (0, 2, 1, 3):
+                second_copy(h, m, k).start()
+
+    def stage4(m):
+        for h in range(2):
+            c = place[1 - h]
+            second_copy(h, m, 0).wait_recv()
+            in2[h, m, 0] = in2[h, m, 0] + mid[h, m, lax.rem(c + 1, 4), 0]
+            second_copy(h, m, 4).start()
+            second_copy(h, m, 2).wait_recv()
+            in2[h, m, 2] = in2[h, m, 2] + mid[h, m, lax.rem(c + 3, 4), 1]
+            second_copy(h, m, 5).start()
+
+    def stage5(m):
+        for h in range(2):
+            c = place[1 - h]
+            for k in (1, 3, 4, 5):
+                second_copy(h, m, k).wait_recv()
+            low[h, m, 0] = mid[h, m, c, 0] + in2[h, m, 3] + in2[h, m, 4]
+            low[h, m, 1] = mid[h, m, c, 1] + in2[h, m, 1] + in2[h, m, 5]
+            z_copy(h, m).start()
+
+    def owned(m):
+        outs = []
+        for h in range(2):
+            z_copy(h, m).wait_recv()
+            total = low[h, m, zh] + inz[h, m]
+            outs.append(total * st_ref[...] * sg_ref[:, h * 128 : (h + 1) * 128])
+        return outs
+
+    lane = lax.broadcasted_iota(jnp.int32, (32, 128), 1)
+
+    def stage6(m):
+        left, right = owned(m)
+        peak = jnp.max(jnp.maximum(jnp.abs(left), jnp.abs(right)), axis=1, keepdims=True)
+        pm[...] = jnp.where(lane == m - 1, peak, pm[...])
+
+    pm[...] = jnp.zeros_like(pm)
+    compute(0, g_ref)
+    stage1(0)
+
+    def step(i, carry):
+        @pl.when(i < mats)
+        def _():
+            permute(i)
+            compute(i, q_ref)
+            stage1(i)
+
+        for lag, stage in ((1, stage2), (2, stage3), (3, stage4), (4, stage5)):
+            @pl.when((i >= lag) & (i < mats + lag))
+            def _(stage=stage, lag=lag):
+                stage(i - lag)
+
+        @pl.when((i >= 6) & (i < mats + 5))
+        def _():
+            stage6(i - 5)
+
+        @pl.when(i == 5)
+        def _():
+            left, right = owned(0)
+            obs_ref[:, :128] = left
+            obs_ref[:, 128:] = right
+
+        return carry
+
+    lax.fori_loop(1, mats + 5, step, 0)
+
+    def tile_copy(d):
+        return pltpu.make_async_remote_copy(
+            src_ref=pm, dst_ref=pmin.at[d - 1], send_sem=sendt.at[d - 1],
+            recv_sem=recvt.at[d - 1], device_id={"tile": lax.rem(t + d, 8)},
+            device_id_type=MESH,
+        )
+
+    for d in range(1, 8):
+        tile_copy(d).start()
+
+    def drain(m, carry):
+        for h in range(2):
+            for k in range(6):
+                first_copy(h, m, k).wait_send()
+                second_copy(h, m, k).wait_send()
+            z_copy(h, m).wait_send()
+        return carry
+
+    lax.fori_loop(0, mats, drain, 0)
+    best = pm[...]
+    for d in range(1, 8):
+        tile_copy(d).wait_recv()
+        best = jnp.maximum(best, pmin[d - 1])
+    peak_ref[...] = best
+    for d in range(1, 8):
+        tile_copy(d).wait_send()
+
+
+def scan(yt, g, order, st, sg):
+    perms = order.shape[0]
+    mats = perms + 1
+    vmem = pl.BlockSpec(memory_space=pltpu.VMEM)
+    f32 = jnp.float32
+    dma = pltpu.SemaphoreType.DMA
+    return pl.pallas_call(
+        scan_kernel,
+        out_shape=(
+            jax.ShapeDtypeStruct((32, 256), f32),
+            jax.ShapeDtypeStruct((32, 128), f32),
+        ),
+        in_specs=[vmem] * 5,
+        out_specs=(vmem, vmem),
+        scratch_shapes=[
+            pltpu.VMEM(g.shape, jnp.bfloat16),
+            pltpu.VMEM((2, mats, 4, 2, 4, 32, 128), f32),
+            pltpu.VMEM((2, mats, 6, 4, 32, 128), f32),
+            pltpu.VMEM((2, mats, 4, 2, 32, 128), f32),
+            pltpu.VMEM((2, mats, 6, 32, 128), f32),
+            pltpu.VMEM((2, mats, 2, 32, 128), f32),
+            pltpu.VMEM((2, mats, 32, 128), f32),
+            pltpu.VMEM((32, 128), f32),
+            pltpu.VMEM((7, 32, 128), f32),
+            dma((2, mats, 6)), dma((2, mats, 6)),
+            dma((2, mats, 6)), dma((2, mats, 6)),
+            dma((2, mats)), dma((2, mats)),
+            dma((7,)), dma((7,)),
+        ],
+        compiler_params=pltpu.CompilerParams(
+            collective_id=0, has_side_effects=True, vmem_limit_bytes=48 * 1024 * 1024
+        ),
+    )(yt, g, order, st, sg)
 
 
 def shards(traits, covariates, genotypes, shuffles):
@@ -120,21 +365,10 @@
     scale_geno = lax.rsqrt(mean_geno + epsilon)
     factor_z = math.sqrt(samples - C - 2) / samples
     own_scale = lax.dynamic_slice_in_dim(scale_traits, own_index * share_rows, share_rows, 0)
-
-    def owned_scores(trait_rows):
-        owned = sum_at_owner(cross_local(trait_rows, rg_rows), "samp", 0)
-        return owned * own_scale[:, None] * scale_geno[None, :] * factor_z
-
-    observed = owned_scores(rt_rows)
-    peaks = []
-    for perm_id in range(shuffles.shape[0]):
-        local_order = shuffles[perm_id] - own_index * local_rows
-        shuffled = jnp.take(rt_rows, local_order, axis=0)
-        peak = jnp.max(jnp.abs(owned_scores(shuffled)), axis=1)
-        peaks.append(peak)
-    perm_max = jnp.stack(peaks, axis=0)
-    perm_max = taken_together(perm_max, "tile")
-    return (observed, perm_max)
+    observed, peaks = scan(
+        rt_rows.T, rg_rows, shuffles, own_scale[:, None] * factor_z, scale_geno[None, :]
+    )
+    return (observed, peaks[:, : shuffles.shape[0]].T)
 
 
 def solution(mesh):

time: 308 us -> 144 us (0.47)
  waiting for transfers between devices: 108 us -> 20.6 us
  starting transfers between devices: 80.2 us -> 7.74 us
  Pallas kernels: 0 us -> 66.3 us
  local copies, waits for them, and re-layouts: 36.3 us -> 6.65 us
  matrix products: 31.8 us -> 7.41 us
  other arithmetic: 16.4 us -> 7.63 us
  blocking collectives: 33 us -> 26 us
    all_to_all x8 -> x0, waiting for transfers between devices: 93.4 us -> none  [sum_at_owner(): lax.all_to_all(in_blocks(value, dim, count), axis, 0, 0, tiled=True)]
    all_to_all x8 -> x0, starting transfers between devices: 72.4 us -> none  [sum_at_owner(): lax.all_to_all(in_blocks(value, dim, count), axis, 0, 0, tiled=True)]
    pallas_call x0 -> x1, Pallas kernels: none -> 66.3 us  [scan(): pl.pallas_call(scan_kernel, out_shape=(jax.ShapeDtypeStruct((32, 256), f3...]
    gather x6 -> x0, local copies, waits for them, and re-layouts: 32.2 us -> none  [shards(): shuffled = jnp.take(rt_rows, local_order, axis=0)]
    dot_general x10 -> x3, matrix products: 27.9 us -> 3.42 us  [cross_local(): lax.dot_general(left, right, (((0,), (0,)), ((), ())), preferred_element_...]
    all_to_all x1, blocking collectives: 33 us -> 26 us  [sum_at_owner(): lax.all_to_all(in_blocks(value, dim, count), axis, 0, 0, tiled=True)]
    reduce_sum x8 -> x1, other arithmetic: 6.75 us -> 0.12 us  [sum_at_owner(): return jnp.sum(blocks, axis=0)]
    all_to_all x2, waiting for transfers between devices: 14.3 us -> 20.6 us  [copy_for_each(): return lax.all_to_all(copies, axis, split_axis=0, concat_axis=0, tiled=True)]
  transfers between devices with their start and end apart: 10 -> 2, of which waited for: 10 -> 2; matrix products, arithmetic and copies ran while one was open for 21% -> 2% of each run, Pallas kernels for 0% -> 0%
where the time goes in v1:
time: 144 us; the launch traced here: 143 us
  Pallas kernels  66.3 us (46%)
  blocking collectives  26 us (18%)
  waiting for transfers between devices  20.6 us (14%)
  starting transfers between devices  7.74 us (5%)
  other arithmetic  7.63 us (5%)
  matrix products  7.41 us (5%)
  local copies, waits for them, and re-layouts  6.65 us (5%)
    pallas_call x1, Pallas kernels, scan(): pl.pallas_call(scan_kernel, out_shape=(jax.ShapeDtypeStruct((32, 256), f3...  66.3 us
    all_to_all x1, blocking collectives, sum_at_owner(): lax.all_to_all(in_blocks(value, dim, count), axis, 0, 0, tiled=True)  26 us
    all_to_all x2, waiting for transfers between devices, copy_for_each(): return lax.all_to_all(copies, axis, split_axis=0, concat_axis=0, tiled=True)  20.6 us
    all_to_all x2, starting transfers between devices, copy_for_each(): return lax.all_to_all(copies, axis, split_axis=0, concat_axis=0, tiled=True)  7.74 us
    unnamed x13, local copies, waits for them, and re-layouts  3.89 us
    another operation x3, other arithmetic, shards(): factor = jnp.linalg.cholesky(gram)  3.68 us
    dot_general x3, matrix products, cross_local(): lax.dot_general(left, right, (((0,), (0,)), ((), ())), preferred_element_...  3.42 us
    another operation x2, other arithmetic, cholesky_solve(): lax.linalg.triangular_solve(factor, first, left_side=True, lower=True, tr...  3.18 us
  transfers between devices with their start and end apart: 2, of which 2 were waited for; matrix products, arithmetic and copies ran while one was open for 2% of the time, Pallas kernels for 0%

profile of v1, /device:TPU:1, one launch (start us, length us, event | category | flops | bytes accessed | tf_op | source)
XLA Modules:
  0.0 143.2 jit_solution(7453937060700265659)
XLA Ops:
  0.7 1.1 fusion.10
  1.9 2.1 %fusion.8 = f32[33,1024]{1,0:T(8,128)S(1)} fusion(bf16[1024,1024]{1,0:T(8,128)(2,1)} %param.4, bf16[1024,32]{0,1:T(8,128)(2,1)} %param.5), kind=kOutput, calls=%fused_computation.14 | convolution fusion | flops 69206016 | bytes 2297856 | tf_op jit(solution)/shard_map/dot_general | solution.py:84
  4.1 0.2 fusion.2
  4.3 0.1 concatenate.10
  4.4 0.3 all_to_all.14
  4.7 26.0 %all_to_all.21 = f32[32,1,1355]{2,1,0:T(1,128)S(1)} all-to-all(f32[32,1,1355]{2,1,0:T(1,128)S(1)} %all_to_all.14), channel_id=1, replica_groups=mesh['samp'=32,'tile'=8] {'samp'}, dimensions={0} | all-to-all | bytes 346880 | tf_op jit(solution)/shard_map/all_to_all | solution.py:46
  30.7 0.1 reduce_sum.36
  30.9 0.8 broadcast_in_dim.13
  31.6 3.9 %all-to-all-start.1 = ((f32[32,1,1355]{2,1,0:T(1,128)}), f32[32,1,1355]{2,1,0:T(1,128)S(1)}, u32[]{:S(2)}, u32[]{:S(2)}) async-start(f32[32,1,1355]{2,1,0:T(1,128)} %broadcast_in_dim.13), calls=%async_computation.1 | async-start | bytes 360448 | tf_op jit(solution)/shard_map/all_to_all | solution.py:31
  35.5 2.6 %copy.21 = bf16[1024,1024]{0,1:T(8,128)(2,1)} copy(bf16[1024,1024]{1,0:T(8,128)(2,1)S(1)} %copy-done.1) | data formatting | bytes 4194304 | tf_op args[0]
  38.1 9.0 %all-to-all-done.1 = f32[32,1,1355]{2,1,0:T(1,128)S(1)} async-done(((f32[32,1,1355]{2,1,0:T(1,128)}), f32[32,1,1355]{2,1,0:T(1,128)S(1)}, u32[]{:S(2)}, u32[]{:S(2)}) %all-to-all-start.1) | async-done | bytes 173472 | tf_op jit(solution)/shard_map/all_to_all | solution.py:31
  47.1 0.4 reduce.8
  47.6 0.2 reshape.57
  47.7 0.1 slice.51
  48.0 0.1 reshape.58
  48.2 3.0 %cholesky.16 = f32[33,33]{1,0:T(8,128)S(1)} custom-call(f32[33,33]{1,0:T(8,128)S(1)} %fusion.19), custom_call_target="Cholesky" | custom-call | tf_op jit(solution)/shard_map/jit(cholesky)/cholesky | solution.py:347
  51.2 0.6 compare_reduce_fusion
  51.9 0.7 fusion.12
  52.5 2.5 %custom-call.12 = f32[1,33,33]{1,2,0:T(8,128)S(1)} custom-call(f32[1,33,33]{2,1,0:T(8,128)S(1)} %fusion.12), custom_call_target="InvertDiagBlocksLowerTriangular" | custom-call | tf_op jit(solution)/shard_map/triangular_solve | solution.py:80
  55.1 0.4 fusion.17
  55.4 0.3 convolution_convert_fusion
  55.7 0.2 fusion.14
  56.0 0.2 convolution_convert_fusion.1
  56.1 0.4 multiply_reduce_fusion.1
  56.6 2.6 %multiply_reduce_fusion = (f32[1024]{0:T(1024)S(1)}, bf16[1024,1024]{1,0:T(8,128)(2,1)S(1)}) fusion(bf16[1024,1024]{0,1:T(8,128)(2,1)} %copy.21, bf16[33,1024]{1,0:T(8,128)(2,1)S(1)} %convolution_convert_fusion, bf16[1024,32]{0,1:T(8,128)(2,1)S(1)} %copy-done.4), kind=kOutput, calls=%fused_computation | convolution fusion | flops 74447872 | bytes 4331520 | tf_op jit(solution)/shard_map/dot_general | solution.py:350
  59.1 0.7 broadcast_in_dim.14
  59.9 3.9 %all-to-all-start.2 = ((f32[32,1,1280]{2,1,0:T(1,128)}), f32[32,1,1280]{2,1,0:T(1,128)S(1)}, u32[]{:S(2)}, u32[]{:S(2)}) async-start(f32[32,1,1280]{2,1,0:T(1,128)} %broadcast_in_dim.14), calls=%async_computation.2 | async-start | bytes 327680 | tf_op jit(solution)/shard_map/all_to_all | solution.py:31
  63.7 11.6 %all-to-all-done.2 = f32[32,1,1280]{2,1,0:T(1,128)S(1)} async-done(((f32[32,1,1280]{2,1,0:T(1,128)}), f32[32,1,1280]{2,1,0:T(1,128)S(1)}, u32[]{:S(2)}, u32[]{:S(2)}) %all-to-all-start.2) | async-done | bytes 163872 | tf_op jit(solution)/shard_map/all_to_all | solution.py:31
  75.3 0.1 reduce_sum.39
  75.6 66.3 %shard_map.59 = (f32[32,256]{1,0:T(8,128)S(1)}, f32[32,128]{1,0:T(8,128)S(1)}) custom-call(bf16[1024,1024]{1,0:T(8,128)(2,1)S(1)} %get-tuple-element.15.yt_ref, bf16[1024,256]{1,0:T(8,128)(2,1)S(1)} %get-tuple-element.17.g_ref, s32[6,1024]{1,0:T(8,128)S(1)} %copy-done, f32[32,1]{1,0:T(8,128)S(1)} %copy.26.st_ref, f32[1,256]{1,0:T(1,128)S(1)} %bitcast.29), custom_call_target="tpu_custom_call" | custom-call | tf_op jit(solution)/shard_map/pallas_call | solution.py:305
  141.9 0.7 copy.27
  142.6 0.6 copy.34
  (27 shorter events, 0.6 us)
Async XLA Ops:
  0.6 3.4 %copy-start.3 = (bf16[1024,32]{0,1:T(8,128)(2,1)S(1)}, bf16[1024,32]{0,1:T(8,128)(2,1)}, u32[]{:S(2)}) copy-start(bf16[1024,32]{0,1:T(8,128)(2,1)} %param.5) | copy-start | bytes 196612
  0.6 3.4 %copy-start.2 = (s32[1024,256]{1,0:T(8,128)S(1)}, s32[1024,256]{1,0:T(8,128)}, u32[]{:S(2)}) copy-start(s32[1024,256]{1,0:T(8,128)} %param.6) | copy-start | bytes 3145732
  4.0 31.5 %copy-start.1 = (bf16[1024,1024]{1,0:T(8,128)(2,1)S(1)}, bf16[1024,1024]{1,0:T(8,128)(2,1)}, u32[]{:S(2)}) copy-start(bf16[1024,1024]{1,0:T(8,128)(2,1)} %param.4) | copy-start | bytes 6291460
  31.6 15.5 %all-to-all-start.1 = ((f32[32,1,1355]{2,1,0:T(1,128)}), f32[32,1,1355]{2,1,0:T(1,128)S(1)}, u32[]{:S(2)}, u32[]{:S(2)}) async-start(f32[32,1,1355]{2,1,0:T(1,128)} %broadcast_in_dim.13), calls=%async_computation.1 | async-start | bytes 360448 | tf_op jit(solution)/shard_map/all_to_all | solution.py:31
  38.1 18.0 %copy-start.4 = (bf16[1024,32]{0,1:T(8,128)(2,1)S(1)}, bf16[1024,32]{0,1:T(8,128)(2,1)}, u32[]{:S(2)}) copy-start(bf16[1024,32]{0,1:T(8,128)(2,1)} %param.5) | copy-start | bytes 196612
  56.5 19.1 %copy-start = (s32[6,1024]{1,0:T(8,128)S(1)}, s32[6,1024]{1,0:T(8,128)}, u32[]{:S(2)}) copy-start(s32[6,1024]{1,0:T(8,128)} %order_ref.1) | copy-start | bytes 73732
  59.9 15.4 %all-to-all-start.2 = ((f32[32,1,1280]{2,1,0:T(1,128)}), f32[32,1,1280]{2,1,0:T(1,128)S(1)}, u32[]{:S(2)}, u32[]{:S(2)}) async-start(f32[32,1,1280]{2,1,0:T(1,128)} %broadcast_in_dim.14), calls=%async_computation.2 | async-start | bytes 327680 | tf_op jit(solution)/shard_map/all_to_all | solution.py:31

commit v2 on v1

v2 whole, which is shorter than its diff:
```python
import functools
import math

import jax
import jax.numpy as jnp
from jax import lax
from jax.experimental import pallas as pl
from jax.experimental.pallas import tpu as pltpu
from jax.sharding import PartitionSpec as P

C = 32


epsilon = 1e-05
MESH = pl.DeviceIdType.MESH
f32 = jnp.float32
bf16 = jnp.bfloat16


def exact_dot(a, b):
    return jnp.dot(a, b, preferred_element_type=f32, precision=lax.Precision.HIGHEST)


def across(a, b):
    return lax.dot_general(a, b, (((1,), (1,)), ((), ())), preferred_element_type=f32)


def iota(shape, dim):
    return lax.broadcasted_iota(jnp.int32, shape, dim)


def scan_kernel(
    y_ref, cov_ref, geno_ref, order_ref, obs_ref, peak_ref,
    yt, q, xt, tps, part, in1, mid, in2, low, inz, lowin, agu, tt,
    lhs, vst, corr, st_ref, sg_ref, pm, pmin,
    send1, recv1, send2, recv2, sendz, recvz, sendx, recvx, sendt, recvt,
    *, samples,
):
    perms = order_ref.shape[0]
    mats = perms + 1
    aux = mats
    rows = y_ref.shape[0]
    s = lax.axis_index("samp")
    t = lax.axis_index("tile")
    x = lax.rem(s, 4)
    zh = lax.rem(s // 4, 2)
    y = s // 8
    core = lax.rem(t, 2)
    zl = t // 2
    base = s * rows

    def at_x(v):
        return s - x + lax.rem(v, 4)

    def at_y(v):
        return lax.rem(v, 4) * 8 + lax.rem(s, 8)

    z_peer = s + 4 - 8 * zh
    place = (x, y)
    peers = ((at_x(x + 1), at_x(x + 3)), (at_y(y + 1), at_y(y + 3)))

    barrier = pltpu.get_barrier_semaphore()
    for peer in (*peers[0], *peers[1], at_y(y + 2), z_peer):
        pl.semaphore_signal(barrier, inc=1, device_id={"samp": peer}, device_id_type=MESH)
    for d in range(1, 8):
        pl.semaphore_signal(
            barrier, inc=1, device_id={"tile": lax.rem(t + d, 8)}, device_id_type=MESH
        )

    def remote(src, dst, send, recv, peer):
        return pltpu.make_async_remote_copy(
            src_ref=src, dst_ref=dst, send_sem=send, recv_sem=recv,
            device_id={"samp": peer}, device_id_type=MESH,
        )

    def to_tile(src, dst, k, d):
        return pltpu.make_async_remote_copy(
            src_ref=src, dst_ref=dst, send_sem=sendt.at[k, d - 1], recv_sem=recvt.at[k, d - 1],
            device_id={"tile": lax.rem(t + d, 8)}, device_id_type=MESH,
        )

    def first_copy(h, m, k):
        c = place[h]
        blk = lax.rem(c + (2, 1, 2, 3, 1, 3)[k], 4)
        uv = (0, 1, 1, 0, 0, 1)[k]
        src = part.at[h, m, blk, uv]
        if k >= 4:
            src = in1.at[h, m, 0 if k == 4 else 2]
        return remote(
            src, in1.at[h, m, k], send1.at[h, m, k], recv1.at[h, m, k],
            peers[h][(0, 0, 1, 1, 0, 1)[k]],
        )

    def second_copy(h, m, k):
        c = place[1 - h]
        blk = lax.rem(c + (2, 1, 2, 3, 1, 3)[k], 4)
        uv = (0, 1, 1, 0, 0, 1)[k]
        src = mid.at[h, m, blk, uv]
        if k >= 4:
            src = in2.at[h, m, 0 if k == 4 else 2]
        return remote(
            src, in2.at[h, m, k], send2.at[h, m, k], recv2.at[h, m, k],
            peers[1 - h][(0, 0, 1, 1, 0, 1)[k]],
        )

    def z_copy(h, m):
        return remote(
            low.at[h, m, 1 - zh], inz.at[h, m], sendz.at[h, m], recvz.at[h, m], z_peer
        )

    def compute(m):
        def block(yb, carry):
            lines = yt[pl.ds(pl.multiple_of(yb * 256, 256), 256), :]
            out = jnp.dot(lines, q[m, :, :256], preferred_element_type=f32)
            for z in range(2):
                for xb in range(4):
                    at = (z * 4 + xb) * 32
                    part[0, m, xb, z, yb] = out[at : at + 32, :128]
                    part[1, m, yb, z, xb] = out[at : at + 32, 128:]
            return carry

        lax.fori_loop(0, 4, block, 0)

    def permute(m):
        order = order_ref[pl.ds(m - 1, 1), :] - base

        def block(jb, carry):
            target = iota((256, rows), 0) + jb * 256
            hot = jnp.where(target == order, 1.0, 0.0).astype(bf16)
            moved = jnp.dot(hot, q[0], preferred_element_type=f32)
            q[m, pl.ds(pl.multiple_of(jb * 256, 256), 256), :] = moved.astype(bf16)
            return carry

        lax.fori_loop(0, 4, block, 0)

    def stage1(m, halves=(0, 1)):
        for k in (0, 2, 1, 3):
            for h in halves:
                first_copy(h, m, k).start()

    def stage2(m, halves=(0, 1)):
        for h in halves:
            c = place[h]
            first_copy(h, m, 0).wait_recv()
            in1[h, m, 0] = in1[h, m, 0] + part[h, m, lax.rem(c + 1, 4), 0]
            first_copy(h, m, 4).start()
            first_copy(h, m, 2).wait_recv()
            in1[h, m, 2] = in1[h, m, 2] + part[h, m, lax.rem(c + 3, 4), 1]
            first_copy(h, m, 5).start()

    def stage3(m, halves=(0, 1)):
        for h in halves:
            c = place[h]
            for k in (1, 3, 4, 5):
                first_copy(h, m, k).wait_recv()
            mid[h, m, :, 0] = part[h, m, c, 0] + in1[h, m, 3] + in1[h, m, 4]
            mid[h, m, :, 1] = part[h, m, c, 1] + in1[h, m, 1] + in1[h, m, 5]
            for k in (0, 2, 1, 3):
                second_copy(h, m, k).start()

    def stage4(m, halves=(0, 1)):
        for h in halves:
            c = place[1 - h]
            second_copy(h, m, 0).wait_recv()
            in2[h, m, 0] = in2[h, m, 0] + mid[h, m, lax.rem(c + 1, 4), 0]
            second_copy(h, m, 4).start()
            second_copy(h, m, 2).wait_recv()
            in2[h, m, 2] = in2[h, m, 2] + mid[h, m, lax.rem(c + 3, 4), 1]
            second_copy(h, m, 5).start()

    def second_sum(h, m):
        c = place[1 - h]
        for k in (1, 3, 4, 5):
            second_copy(h, m, k).wait_recv()
        low[h, m, 0] = mid[h, m, c, 0] + in2[h, m, 3] + in2[h, m, 4]
        low[h, m, 1] = mid[h, m, c, 1] + in2[h, m, 1] + in2[h, m, 5]

    def stage5(m):
        for h in range(2):
            second_sum(h, m)
            z_copy(h, m).start()


    def aux_parts():
        def line(m, carry):
            out = jnp.dot(xt[...], q[m], preferred_element_type=f32)
            for j in range(4):
                for k in range(3):
                    part[1, aux, m // 2, lax.rem(m, 2), j, 8 + 8 * k : 16 + 8 * k] = out[
                        8 * j : 8 * j + 8, 128 * k : 128 * k + 128
                    ]
            return carry

        lax.fori_loop(0, mats, line, 0)
        ends = jnp.dot(xt[32:48, :], q[0], preferred_element_type=f32)[:8]
        squares = q[0, :, :256].astype(f32)
        squares = jnp.sum(squares * squares, axis=0, keepdims=True)
        second = iota((8, 128), 0) == 1
        for k in range(3):
            piece = ends[:, 128 * k : 128 * k + 128]
            if k < 2:
                piece = jnp.where(second, squares[:, 128 * k : 128 * k + 128], piece)
            part[1, aux, 3, 1, 0, 8 + 8 * k : 16 + 8 * k] = piece
        for j in range(1, 4):
            part[1, aux, 3, 1, j, 8:32] = jnp.zeros((24, 128), f32)
        group = iota((rows, 128), 1) // 32
        last = jnp.where(
            core == 0,
            q[3, :, 256:].astype(f32),
            jnp.where(iota((rows, 128), 1) == 96, 1.0, 0.0),
        )
        picked = last
        for k in range(3):
            picked = jnp.where(group == k, q[4 * core + k, :, 256:].astype(f32), picked)
        picked = picked.astype(bf16)
        square_at = (iota((256, 128), 1) == 97) & (core == 1)

        def block(yb, carry):
            lines = yt[pl.ds(pl.multiple_of(yb * 256, 256), 256), :]
            out = jnp.dot(lines, picked, preferred_element_type=f32)
            wide = lines.astype(f32)
            out = jnp.where(square_at, jnp.sum(wide * wide, axis=1, keepdims=True), out)
            tps[pl.ds(pl.multiple_of(yb * 8, 8), 8)] = out.reshape(8, 32, 128)
            return carry

        lax.fori_loop(0, 4, block, 0)
        mine = tps[:, pl.ds(pl.multiple_of(zl * 8, 8), 8), :]
        part[1, aux, :, :, :, 0:8] = mine.reshape(4, 2, 4, 8, 128)

    def both_copy():
        return remote(low.at[1, aux], lowin, sendx.at[0], recvx.at[0], z_peer)

    def along_y(d):
        return remote(
            agu.at[x, y], agu.at[x, y], sendx.at[d], recvx.at[d], at_y(y + d)
        )

    def along_x(k):
        if k < 2:
            ref = agu.at[x]
        elif k == 2:
            ref = agu.at[lax.rem(x + 3, 4), pl.ds(0, 2)]
        else:
            ref = agu.at[lax.rem(x + 1, 4), pl.ds(2, 2)]
        return remote(ref, ref, sendx.at[4 + k], recvx.at[4 + k], peers[0][k % 2])

    def aux_low():
        second_sum(1, aux)
        both_copy().start()

    def aux_total():
        both_copy().wait_recv()
        total = low[1, aux] + lowin[...]
        agu[x, y] = total[:, 8:]
        for d in range(1, 4):
            along_y(d).start()
        tt[t] = jnp.where(zh == 0, total[0, :8], total[1, :8])
        for d in range(1, 8):
            to_tile(tt.at[t], tt.at[t], 0, d).start()

    def aux_row():
        for d in range(1, 4):
            along_y(d).wait_recv()
        along_x(0).start()
        along_x(1).start()

    def aux_pass():
        along_x(0).wait_recv()
        along_x(1).wait_recv()
        along_x(2).start()
        along_x(3).start()

    def solve():
        along_x(2).wait_recv()
        along_x(3).wait_recv()
        for d in range(1, 8):
            to_tile(tt.at[t], tt.at[t], 0, d).wait_recv()
        lane = iota((32, 128), 1)
        row = iota((32, 128), 0)
        lane8 = iota((8, 128), 1)
        row8 = iota((8, 128), 0)

        def eight(k):
            return agu[0, 3, 1, 8 * k : 8 * k + 8]

        def product(m, k):
            return agu[:, m // 2, m % 2, 8 * k : 8 * k + 8].reshape(32, 128)

        sums = eight(2)[0:1]
        sum_column = jnp.sum(jnp.where(lane == row, sums, 0.0), axis=1, keepdims=True)
        sum_rows = jnp.where(
            row8 == 0, jnp.where(lane8 < 32, sums, jnp.where(lane8 == 32, samples, 0.0)), 0.0
        )
        ones_g = jnp.concatenate([eight(0), eight(1)], axis=1)
        ones_rows = jnp.where(iota((8, 256), 0) == 0, ones_g, 0.0)

        def gram_of(m):
            body = jnp.where(lane < 32, product(m, 2), jnp.where(lane == 32, sum_column, 0.0))
            return jnp.concatenate([body, sum_rows], axis=0)

        def geno_of(m):
            body = jnp.concatenate([product(m, 0), product(m, 1)], axis=1)
            return jnp.concatenate([body, ones_rows], axis=0)

        trait_sums = [
            jnp.concatenate([tt[2 * k + c] for k in range(4)], axis=0) for c in range(2)
        ]
        ones_y = trait_sums[1][:, 96:97]
        squares_y = trait_sums[1][:, 97:98]

        def trait_of(m):
            own = trait_sums[m // 4]
            k = m % 4
            if k:
                own = pltpu.roll(own, 128 - 32 * k, 1)
            return jnp.where(lane < 32, own, jnp.where(lane == 32, ones_y, 0.0))

        gram = gram_of(0)
        inv = gram
        lane40 = iota((40, 128), 1)
        row40 = iota((40, 128), 0)
        for k in range(C + 1):
            pivot = inv[k : k + 1, k : k + 1]
            line = jnp.where(lane8[:1] == k, 1.0, inv[k : k + 1, :]) / pivot
            column = inv[:, k : k + 1]
            rest = jnp.where(lane40 == k, 0.0, inv)
            inv = jnp.where(row40 == k, line, rest - column * line)
        pad128 = jnp.zeros((88, 128), f32)
        pad256 = jnp.zeros((88, 256), f32)
        geno0 = geno_of(0)
        coef_g = exact_dot(inv, jnp.concatenate([geno0, pad256], axis=0))
        coef_g = coef_g.astype(bf16).astype(f32)
        trait0 = trait_of(0)
        coef_t = exact_dot(trait0, jnp.concatenate([inv, pad128], axis=0))
        coef_t = coef_t.astype(bf16).astype(f32)
        for m in range(mats):
            lhs[m * 40 : m * 40 + 40] = gram_of(m)
            lhs[mats * 40 + m * 32 : mats * 40 + m * 32 + 32] = trait_of(m)
        out = exact_dot(lhs[...], jnp.concatenate([coef_g, pad256], axis=0))
        for m in range(mats):
            left = geno_of(m) - out[m * 40 : m * 40 + 40]
            vst[:40, m * 256 : m * 256 + 256] = left
            vst[40:, m * 256 : m * 256 + 256] = pad256
            if m == 0:
                squares_g = ones_g[1:2] - jnp.sum(
                    coef_g * (geno0 + left), axis=0, keepdims=True
                )
        more = exact_dot(coef_t, vst[...])
        for m in range(mats):
            at = mats * 40 + m * 32
            corr[m] = out[at : at + 32] + more[:, m * 256 : m * 256 + 256]
        back = exact_dot(coef_t, jnp.concatenate([gram, pad128], axis=0))
        squares_t = squares_y - jnp.sum(coef_t * (2.0 * trait0 - back), axis=1, keepdims=True)
        mean_t = jnp.maximum(squares_t, 0.0) / samples
        mean_g = jnp.maximum(squares_g, 0.0) / samples
        factor_z = math.sqrt(samples - C - 2) / samples
        st_ref[...] = jnp.broadcast_to(lax.rsqrt(mean_t + epsilon) * factor_z, (32, 128))
        sg_ref[...] = jnp.broadcast_to(lax.rsqrt(mean_g + epsilon), (8, 256))

    def owned(m):
        outs = []
        for h in range(2):
            z_copy(h, m).wait_recv()
            cols = slice(h * 128, h * 128 + 128)
            total = low[h, m, zh] + inz[h, m] - corr[m, :, cols]
            outs.append(total * st_ref[...] * sg_ref[0:1, cols])
        return outs

    spread = jnp.where(lax.rem(iota((32, 128), 1), 32) == iota((32, 128), 0), 1.0, 0.0)
    spread = spread.astype(bf16)
    for b in range(4):
        at = slice(b * 256, b * 256 + 256)
        q[0, at, :256] = geno_ref[at, :].astype(f32).astype(bf16)
        q[0, at, 256:] = jnp.dot(
            cov_ref[at, :], spread, preferred_element_type=f32
        ).astype(bf16)
    pick = jnp.where(iota((48, 32), 0) == iota((48, 32), 1), 1.0, 0.0).astype(bf16)
    lines = across(pick, cov_ref[...])
    xt[...] = jnp.where(iota((48, rows), 0) == 32, 1.0, lines).astype(bf16)
    eye = jnp.where(iota((256, 256), 0) == iota((256, 256), 1), 1.0, 0.0).astype(bf16)

    def flip(b, carry):
        at = pl.ds(pl.multiple_of(b * 256, 256), 256)
        yt[at, :] = across(eye, y_ref[:, at]).astype(bf16)
        return carry

    lax.fori_loop(0, 4, flip, 0)

    def early(m, carry):
        @pl.when(m >= 1)
        def _():
            permute(m)

        @pl.when(m < 2)
        def _():
            compute(m)

        @pl.when(m == 0)
        def _():
            pl.semaphore_wait(barrier, 13)

        @pl.when(m < 2)
        def _():
            stage1(m)

        return carry

    lax.fori_loop(0, mats, early, 0)
    aux_parts()
    stage1(aux, (1,))
    stage2(0)

    first_step = 2
    steps = {
        2: (lambda: stage2(aux, (1,)), lambda: stage3(aux, (1,))),
        3: (lambda: stage4(aux, (1,)), aux_low),
        4: (aux_total, aux_row),
        5: (aux_pass, solve),
    }

    def step(i, carry):
        def small(part_of):
            for at, pair in steps.items():
                @pl.when(i == at)
                def _(pair=pair):
                    pair[part_of]()

        small(0)

        @pl.when(i < mats)
        def _():
            compute(i)
            stage1(i)

        @pl.when(i < mats + 1)
        def _():
            stage2(i - 1)

        small(1)

        for lag, stage in ((2, stage3), (3, stage4), (4, stage5)):
            @pl.when((i >= lag) & (i < mats + lag))
            def _(stage=stage, lag=lag):
                stage(i - lag)

        return carry

    lax.fori_loop(first_step, mats + 4, step, 0)

    left, right = owned(0)
    obs_ref[:, :128] = left
    obs_ref[:, 128:] = right
    lane = iota((32, 128), 1)
    best = jnp.zeros((32, 128), f32)
    for m in range(1, mats):
        left, right = owned(m)
        peak = jnp.max(jnp.maximum(jnp.abs(left), jnp.abs(right)), axis=1, keepdims=True)
        best = jnp.where(lane == m - 1, peak, best)
    pm[...] = best
    for d in range(1, 8):
        to_tile(pm, pmin.at[d - 1], 1, d).start()

    def drain(m, carry):
        for h in range(2):
            for k in range(6):
                first_copy(h, m, k).wait_send()
                second_copy(h, m, k).wait_send()
            z_copy(h, m).wait_send()
        return carry

    lax.fori_loop(0, mats, drain, 0)
    for k in range(6):
        first_copy(1, aux, k).wait_send()
        second_copy(1, aux, k).wait_send()
    both_copy().wait_send()
    for d in range(1, 4):
        along_y(d).wait_send()
    for k in range(4):
        along_x(k).wait_send()
    for d in range(1, 8):
        to_tile(tt.at[t], tt.at[t], 0, d).wait_send()
    for d in range(1, 8):
        to_tile(pm, pmin.at[d - 1], 1, d).wait_recv()
        best = jnp.maximum(best, pmin[d - 1])
    peak_ref[...] = best
    for d in range(1, 8):
        to_tile(pm, pmin.at[d - 1], 1, d).wait_send()


def scan(traits, covariates, genotypes, shuffles, samples):
    perms = shuffles.shape[0]
    mats = perms + 1
    rows = traits.shape[0]
    vmem = pl.BlockSpec(memory_space=pltpu.VMEM)
    dma = pltpu.SemaphoreType.DMA
    return pl.pallas_call(
        functools.partial(scan_kernel, samples=samples),
        out_shape=(
            jax.ShapeDtypeStruct((32, 256), f32),
            jax.ShapeDtypeStruct((32, 128), f32),
        ),
        in_specs=[vmem] * 4,
        out_specs=(vmem, vmem),
        scratch_shapes=[
            pltpu.VMEM((1024, rows), bf16),
            pltpu.VMEM((mats, rows, 384), bf16),
            pltpu.VMEM((48, rows), bf16),
            pltpu.VMEM((32, 32, 128), f32),
            pltpu.VMEM((2, mats + 1, 4, 2, 4, 32, 128), f32),
            pltpu.VMEM((2, mats + 1, 6, 4, 32, 128), f32),
            pltpu.VMEM((2, mats + 1, 4, 2, 32, 128), f32),
            pltpu.VMEM((2, mats + 1, 6, 32, 128), f32),
            pltpu.VMEM((2, mats + 1, 2, 32, 128), f32),
            pltpu.VMEM((2, mats, 32, 128), f32),
            pltpu.VMEM((2, 32, 128), f32),
            pltpu.VMEM((4, 4, 2, 24, 128), f32),
            pltpu.VMEM((8, 8, 128), f32),
            pltpu.VMEM((mats * 72, 128), f32),
            pltpu.VMEM((128, mats * 256), f32),
            pltpu.VMEM((mats, 32, 256), f32),
            pltpu.VMEM((32, 128), f32),
            pltpu.VMEM((8, 256), f32),
            pltpu.VMEM((32, 128), f32),
            pltpu.VMEM((7, 32, 128), f32),
            dma((2, mats + 1, 6)), dma((2, mats + 1, 6)),
            dma((2, mats + 1, 6)), dma((2, mats + 1, 6)),
            dma((2, mats)), dma((2, mats)),
            dma((8,)), dma((8,)),
            dma((2, 7)), dma((2, 7)),
        ],
        compiler_params=pltpu.CompilerParams(
            collective_id=0, has_side_effects=True, vmem_limit_bytes=56 * 1024 * 1024
        ),
    )(traits, covariates, genotypes, shuffles)


def shards(traits, covariates, genotypes, shuffles):
    samples = traits.shape[0] * lax.axis_size("samp")
    observed, peaks = scan(traits, covariates, genotypes, shuffles, samples)
    return (observed, peaks[:, : shuffles.shape[0]].T)


def solution(mesh):
    placed = (P("samp", None), P("samp", None), P("samp", "tile"), P(None, "samp"))
    return jax.shard_map(
        shards,
        mesh=mesh,
        in_specs=placed,
        out_specs=(P("samp", "tile"), P(None, "samp")),
        check_vma=False,
    )
```

time: 144 us -> 101 us (0.70)
  Pallas kernels: 66.3 us -> 96.1 us
  blocking collectives: 26 us -> 0 us
  waiting for transfers between devices: 20.6 us -> 0 us
  starting transfers between devices: 7.74 us -> 0 us
  other arithmetic: 7.63 us -> 0 us
  matrix products: 7.41 us -> 0 us
  local copies, waits for them, and re-layouts: 6.65 us -> 4.43 us
    pallas_call x1, Pallas kernels: 66.3 us -> 96.1 us  [scan(): pl.pallas_call(functools.partial(scan_kernel, samples=samples), out_shape...]
    all_to_all x1 -> x0, blocking collectives: 26 us -> none  [sum_at_owner(): lax.all_to_all(in_blocks(value, dim, count), axis, 0, 0, tiled=True)]
    all_to_all x2 -> x0, waiting for transfers between devices: 20.6 us -> none  [copy_for_each(): return lax.all_to_all(copies, axis, split_axis=0, concat_axis=0, tiled=True)]
    all_to_all x2 -> x0, starting transfers between devices: 7.74 us -> none  [copy_for_each(): return lax.all_to_all(copies, axis, split_axis=0, concat_axis=0, tiled=True)]
    another operation x5 -> x0, other arithmetic: 6.86 us -> none  [the longest x3 3.68 us: shards(): factor = jnp.linalg.cholesky(gram)]
    dot_general x5 -> x0, matrix products: 6.37 us -> none  [the longest x3 3.42 us: cross_local(): lax.dot_general(left, right, (((0,), (0,)), ((), ())), preferred_element_...]
    broadcast_in_dim x2 -> x0, local copies, waits for them, and re-layouts: 1.52 us -> none  [copy_for_each(): copies = jnp.broadcast_to(value, (lax.axis_size(axis), *value.shape))]
    unnamed x13 -> x3, local copies, waits for them, and re-layouts: 3.89 us -> 3.71 us
  transfers between devices with their start and end apart: 2 -> 0, of which waited for: 2 -> 0; matrix products, arithmetic and copies ran while one was open for 2% -> 0% of each run, Pallas kernels for 0% -> 0%
where the time goes in v2:
time: 101 us
  Pallas kernels  96.1 us (95%)
  local copies, waits for them, and re-layouts  4.43 us (4%)
    pallas_call x1, Pallas kernels, scan(): pl.pallas_call(functools.partial(scan_kernel, samples=samples), out_shape...  96.1 us
    unnamed x3, local copies, waits for them, and re-layouts  3.71 us

profile of v2, /device:TPU:1, one launch (start us, length us, event | category | flops | bytes accessed | tf_op | source)
XLA Modules:
  0.0 101.2 jit_solution(2945875072134967370)
XLA Ops:
  0.6 1.7 %copy.6.cov_ref = bf16[1024,32]{1,0:T(8,128)(2,1)} copy(bf16[1024,32]{0,1:T(8,128)(2,1)} %param.5) | data formatting | bytes 131072 | tf_op args[1]
  2.3 96.1 %shard_map.59 = (f32[32,256]{1,0:T(8,128)}, f32[32,128]{1,0:T(8,128)}) custom-call(bf16[1024,1024]{1,0:T(8,128)(2,1)} %y_ref.1, bf16[1024,32]{1,0:T(8,128)(2,1)} %copy.6.cov_ref, s32[1024,256]{1,0:T(8,128)} %geno_ref.1, s32[6,1024]{1,0:T(8,128)} %order_ref.1), custom_call_target="tpu_custom_call" | custom-call | tf_op jit(solution)/shard_map/pallas_call | solution.py:496
  98.4 0.7 slice_bitcast_fusion
  99.1 0.7 copy.7
  99.8 1.4 %copy.9 = f32[32,256]{1,0:T(8,128)} copy(f32[32,256]{1,0:T(8,128)} %get-tuple-element.10) | data formatting | bytes 65536

commit v3 on v2

v3 whole, which is shorter than its diff:
```python
import functools
import math

import jax
import jax.numpy as jnp
from jax import lax
from jax.experimental import pallas as pl
from jax.experimental.pallas import tpu as pltpu
from jax.sharding import PartitionSpec as P

C = 32


epsilon = 1e-05
MESH = pl.DeviceIdType.MESH
f32 = jnp.float32
bf16 = jnp.bfloat16


def exact_dot(a, b):
    return jnp.dot(a, b, preferred_element_type=f32, precision=lax.Precision.HIGHEST)


def across(a, b):
    return lax.dot_general(a, b, (((1,), (1,)), ((), ())), preferred_element_type=f32)


def iota(shape, dim):
    return lax.broadcasted_iota(jnp.int32, shape, dim)


def scan_kernel(
    y_ref, cov_ref, geno_ref, order_ref, obs_ref, peak_ref,
    yt, q, xt, tps, part, in1, mid, in2, low, inz, ind, agu, tt,
    lhs, vst, corr, st_ref, sg_ref, pm, pmin,
    send1, recv1, send2, recv2, sendz, recvz, sendd, recvd, sendx, recvx,
    *, samples,
):
    perms = order_ref.shape[0]
    mats = perms + 1
    own = perms
    aux = mats
    ringed = perms - 1
    rows = y_ref.shape[0]
    s = lax.axis_index("samp")
    t = lax.axis_index("tile")
    x = lax.rem(s, 4)
    zh = lax.rem(s // 4, 2)
    y = s // 8
    core = lax.rem(t, 2)
    zl = t // 2
    base = s * rows

    def at_x(d, dz=0):
        return y * 8 + lax.rem(zh + dz, 2) * 4 + lax.rem(x + d, 4)

    def at_y(d, dz=0):
        return lax.rem(y + d, 4) * 8 + lax.rem(zh + dz, 2) * 4 + x

    place = (x, y)
    along = (at_x, at_y)
    apart = [(d, dz) for d in range(4) for dz in range(2) if d or dz]

    barrier = pltpu.get_barrier_semaphore()
    met = [at_y(d, dz) for d, dz in apart] + [at_x(d, dz) for d, dz in apart if d]
    for peer in met:
        pl.semaphore_signal(barrier, inc=1, device_id={"samp": peer}, device_id_type=MESH)
    for d in range(1, 8):
        pl.semaphore_signal(
            barrier, inc=1, device_id={"tile": lax.rem(t + d, 8)}, device_id_type=MESH
        )

    def remote(src, dst, send, recv, peer):
        return pltpu.make_async_remote_copy(
            src_ref=src, dst_ref=dst, send_sem=send, recv_sem=recv,
            device_id={"samp": peer}, device_id_type=MESH,
        )

    def to_tile(src, dst, k, d):
        return pltpu.make_async_remote_copy(
            src_ref=src, dst_ref=dst, send_sem=sendx.at[k], recv_sem=recvx.at[k],
            device_id={"tile": lax.rem(t + d, 8)}, device_id_type=MESH,
        )

    def all_of(ref, send, recv):
        return remote(ref, ref, send, recv, at_x(1))

    def ring_copy(src, buf, h, m, k, c, peers, send, recv):
        blk = lax.rem(c + (2, 2, 1, 3, 1, 3)[k], 4)
        uv = (0, 1, 1, 0, 0, 1)[k]
        ref = buf.at[h, m, k - 4] if k >= 4 else src.at[h, m, blk, uv]
        return remote(
            ref, buf.at[h, m, k], send.at[h], recv.at[h, m, min(k, 2)],
            peers((1, 3, 1, 3, 1, 3)[k]),
        )

    def first_copy(h, m, k):
        return ring_copy(part, in1, h, m, k, place[h], along[h], send1, recv1)

    def second_copy(h, m, k):
        return ring_copy(mid, in2, h, m, k, place[1 - h], along[1 - h], send2, recv2)

    def z_copy(h, m):
        return remote(
            low.at[h, m, 1 - zh], inz.at[h, m], sendz.at[h], recvz.at[h, m], at_x(0, 1)
        )

    def compute(m):
        def block(yb, carry):
            lines = yt[pl.ds(pl.multiple_of(yb * 256, 256), 256), :]
            out = jnp.dot(lines, q[m, :, :256], preferred_element_type=f32)
            for z in range(2):
                for xb in range(4):
                    at = (z * 4 + xb) * 32
                    part[0, m, xb, z, yb] = out[at : at + 32, :128]
                    part[1, m, yb, z, xb] = out[at : at + 32, 128:]
            return carry

        lax.fori_loop(0, 4, block, 0)

    def permute(m):
        order = order_ref[pl.ds(m, 1), :] - base

        def block(jb, carry):
            target = iota((256, rows), 0) + jb * 256
            hot = jnp.where(target == order, 1.0, 0.0).astype(bf16)
            moved = jnp.dot(hot, q[own], preferred_element_type=f32)
            q[m, pl.ds(pl.multiple_of(jb * 256, 256), 256), :] = moved.astype(bf16)
            return carry

        lax.fori_loop(0, 4, block, 0)

    def stage1(m, halves=(0, 1)):
        for k in range(4):
            for h in halves:
                first_copy(h, m, k).start()

    def stage2(m, halves=(0, 1)):
        for h in halves:
            c = place[h]
            for k, d, uv in ((0, 1, 0), (1, 3, 1)):
                first_copy(h, m, k).wait_recv()
                in1[h, m, k] = in1[h, m, k] + part[h, m, lax.rem(c + d, 4), uv]
                first_copy(h, m, k + 4).start()

    def first_sum(h, m):
        c = place[h]
        all_of(in1.at[h, m, pl.ds(2, 4)], send1.at[h], recv1.at[h, m, 2]).wait_recv()
        mid[h, m, :, 0] = part[h, m, c, 0] + in1[h, m, 3] + in1[h, m, 4]
        mid[h, m, :, 1] = part[h, m, c, 1] + in1[h, m, 2] + in1[h, m, 5]

    def stage3(m):
        for h in range(2):
            first_sum(h, m)
            for k in range(4):
                second_copy(h, m, k).start()

    def stage4(m):
        for h in range(2):
            c = place[1 - h]
            for k, d, uv in ((0, 1, 0), (1, 3, 1)):
                second_copy(h, m, k).wait_recv()
                in2[h, m, k] = in2[h, m, k] + mid[h, m, lax.rem(c + d, 4), uv]
                second_copy(h, m, k + 4).start()

    def stage5(m):
        for h in range(2):
            c = place[1 - h]
            all_of(in2.at[h, m, pl.ds(2, 4)], send2.at[h], recv2.at[h, m, 2]).wait_recv()
            low[h, m, 0] = mid[h, m, c, 0] + in2[h, m, 3] + in2[h, m, 4]
            low[h, m, 1] = mid[h, m, c, 1] + in2[h, m, 2] + in2[h, m, 5]
            z_copy(h, m).start()


    def direct(m, halves=(0, 1)):
        for h in halves:
            first_sum(h, m)
            for k, (d, dz) in enumerate(apart):
                blk = lax.rem(place[1 - h] + d, 4)
                remote(
                    mid.at[h, m, blk, lax.rem(zh + dz, 2)], ind.at[h, m - ringed, k],
                    sendd.at[h], recvd.at[h, m - ringed], along[1 - h](d, dz),
                ).start()

    def direct_sum(h, m):
        n = m - ringed
        all_of(ind.at[h, n], sendd.at[h], recvd.at[h, n]).wait_recv()
        total = mid[h, m, place[1 - h], zh]
        for k in range(7):
            total = total + ind[h, n, k]
        return total


    def aux_parts():
        def line(m, carry):
            out = jnp.dot(xt[...], q[m], preferred_element_type=f32)
            for j in range(4):
                for k in range(3):
                    part[1, aux, m // 2, lax.rem(m, 2), j, 8 + 8 * k : 16 + 8 * k] = out[
                        8 * j : 8 * j + 8, 128 * k : 128 * k + 128
                    ]
            return carry

        lax.fori_loop(0, mats, line, 0)
        ends = jnp.dot(xt[32:48, :], q[own], preferred_element_type=f32)[:8]
        squares = q[own, :, :256].astype(f32)
        squares = jnp.sum(squares * squares, axis=0, keepdims=True)
        second = iota((8, 128), 0) == 1
        for k in range(3):
            piece = ends[:, 128 * k : 128 * k + 128]
            if k < 2:
                piece = jnp.where(second, squares[:, 128 * k : 128 * k + 128], piece)
            part[1, aux, 3, 1, 0, 8 + 8 * k : 16 + 8 * k] = piece
        for j in range(1, 4):
            part[1, aux, 3, 1, j, 8:32] = jnp.zeros((24, 128), f32)
        group = iota((rows, 128), 1) // 32
        last = jnp.where(
            core == 0,
            q[3, :, 256:].astype(f32),
            jnp.where(iota((rows, 128), 1) == 96, 1.0, 0.0),
        )
        picked = last
        for k in range(3):
            picked = jnp.where(group == k, q[4 * core + k, :, 256:].astype(f32), picked)
        picked = picked.astype(bf16)
        square_at = (iota((256, 128), 1) == 97) & (core == 1)

        def block(yb, carry):
            lines = yt[pl.ds(pl.multiple_of(yb * 256, 256), 256), :]
            out = jnp.dot(lines, picked, preferred_element_type=f32)
            wide = lines.astype(f32)
            out = jnp.where(square_at, jnp.sum(wide * wide, axis=1, keepdims=True), out)
            tps[pl.ds(pl.multiple_of(yb * 8, 8), 8)] = out.reshape(8, 32, 128)
            return carry

        lax.fori_loop(0, 4, block, 0)
        mine = tps[:, pl.ds(pl.multiple_of(zl * 8, 8), 8), :]
        part[1, aux, :, :, :, 0:8] = mine.reshape(4, 2, 4, 8, 128)

    def aux_total():
        total = direct_sum(1, aux)
        agu[x, y * 2 + zh] = total[8:]
        tt[t] = total[:8]
        for d, dz in apart:
            ref = agu.at[x, y * 2 + zh]
            remote(ref, ref, sendx.at[2], recvx.at[2], at_y(d, dz)).start()
        for d in range(1, 8):
            to_tile(tt.at[t], tt.at[t], 0, d).start()

    def aux_row():
        all_of(agu.at[x, pl.ds(0, 7)], sendx.at[2], recvx.at[2]).wait_recv()
        for d in (1, 3, 2):
            remote(agu.at[x], agu.at[x], sendx.at[3], recvx.at[3], at_x(d)).start()

    def solve():
        all_of(agu.at[pl.ds(0, 3)], sendx.at[3], recvx.at[3]).wait_recv()
        all_of(tt.at[pl.ds(0, 7)], sendx.at[0], recvx.at[0]).wait_recv()
        lane = iota((32, 128), 1)
        row = iota((32, 128), 0)
        lane8 = iota((8, 128), 1)
        row8 = iota((8, 128), 0)

        def eight(k):
            return agu[0, 7, 8 * k : 8 * k + 8]

        def product(m, k):
            return agu[:, m, 8 * k : 8 * k + 8].reshape(32, 128)

        sums = eight(2)[0:1]
        sum_column = jnp.sum(jnp.where(lane == row, sums, 0.0), axis=1, keepdims=True)
        sum_rows = jnp.where(
            row8 == 0, jnp.where(lane8 < 32, sums, jnp.where(lane8 == 32, samples, 0.0)), 0.0
        )
        ones_g = jnp.concatenate([eight(0), eight(1)], axis=1)
        ones_rows = jnp.where(iota((8, 256), 0) == 0, ones_g, 0.0)

        def gram_of(m):
            body = jnp.where(lane < 32, product(m, 2), jnp.where(lane == 32, sum_column, 0.0))
            return jnp.concatenate([body, sum_rows], axis=0)

        def geno_of(m):
            body = jnp.concatenate([product(m, 0), product(m, 1)], axis=1)
            return jnp.concatenate([body, ones_rows], axis=0)

        trait_sums = [
            jnp.concatenate([tt[2 * k + c] for k in range(4)], axis=0) for c in range(2)
        ]
        ones_y = trait_sums[1][:, 96:97]
        squares_y = trait_sums[1][:, 97:98]

        def trait_of(m):
            mine = trait_sums[m // 4]
            k = m % 4
            if k:
                mine = pltpu.roll(mine, 128 - 32 * k, 1)
            return jnp.where(lane < 32, mine, jnp.where(lane == 32, ones_y, 0.0))

        gram = gram_of(own)
        inv = gram
        lane40 = iota((40, 128), 1)
        row40 = iota((40, 128), 0)
        for k in range(C + 1):
            pivot = inv[k : k + 1, k : k + 1]
            line = jnp.where(lane8[:1] == k, 1.0, inv[k : k + 1, :]) / pivot
            column = inv[:, k : k + 1]
            rest = jnp.where(lane40 == k, 0.0, inv)
            inv = jnp.where(row40 == k, line, rest - column * line)
        pad128 = jnp.zeros((88, 128), f32)
        pad256 = jnp.zeros((88, 256), f32)
        geno0 = geno_of(own)
        coef_g = exact_dot(inv, jnp.concatenate([geno0, pad256], axis=0))
        coef_g = coef_g.astype(bf16).astype(f32)
        trait0 = trait_of(own)
        coef_t = exact_dot(trait0, jnp.concatenate([inv, pad128], axis=0))
        coef_t = coef_t.astype(bf16).astype(f32)
        for m in range(mats):
            lhs[m * 40 : m * 40 + 40] = gram_of(m)
            lhs[mats * 40 + m * 32 : mats * 40 + m * 32 + 32] = trait_of(m)
        out = exact_dot(lhs[...], jnp.concatenate([coef_g, pad256], axis=0))
        for m in range(mats):
            left = geno_of(m) - out[m * 40 : m * 40 + 40]
            vst[:40, m * 256 : m * 256 + 256] = left
            vst[40:, m * 256 : m * 256 + 256] = pad256
            if m == own:
                squares_g = ones_g[1:2] - jnp.sum(
                    coef_g * (geno0 + left), axis=0, keepdims=True
                )
        more = exact_dot(coef_t, vst[...])
        for m in range(mats):
            at = mats * 40 + m * 32
            corr[m] = out[at : at + 32] + more[:, m * 256 : m * 256 + 256]
        back = exact_dot(coef_t, jnp.concatenate([gram, pad128], axis=0))
        squares_t = squares_y - jnp.sum(coef_t * (2.0 * trait0 - back), axis=1, keepdims=True)
        mean_t = jnp.maximum(squares_t, 0.0) / samples
        mean_g = jnp.maximum(squares_g, 0.0) / samples
        factor_z = math.sqrt(samples - C - 2) / samples
        st_ref[...] = jnp.broadcast_to(lax.rsqrt(mean_t + epsilon) * factor_z, (32, 128))
        sg_ref[...] = jnp.broadcast_to(lax.rsqrt(mean_g + epsilon), (8, 256))

    def owned(m):
        outs = []
        for h in range(2):
            if m < ringed:
                z_copy(h, m).wait_recv()
                total = low[h, m, zh] + inz[h, m]
            else:
                total = direct_sum(h, m)
            cols = slice(h * 128, h * 128 + 128)
            outs.append((total - corr[m, :, cols]) * st_ref[...] * sg_ref[0:1, cols])
        return outs

    spread = jnp.where(lax.rem(iota((32, 128), 1), 32) == iota((32, 128), 0), 1.0, 0.0)
    spread = spread.astype(bf16)
    for b in range(4):
        at = slice(b * 256, b * 256 + 256)
        q[own, at, :256] = geno_ref[at, :].astype(f32).astype(bf16)
        q[own, at, 256:] = lax.dot_general(
            cov_ref[:, at], spread, (((0,), (0,)), ((), ())), preferred_element_type=f32
        ).astype(bf16)
    xt[:32] = cov_ref[...]
    xt[32:] = jnp.where(iota((16, rows), 0) == 0, 1.0, 0.0).astype(bf16)
    eye = jnp.where(iota((256, 256), 0) == iota((256, 256), 1), 1.0, 0.0).astype(bf16)

    def flip(b, carry):
        at = pl.ds(pl.multiple_of(b * 256, 256), 256)
        yt[at, :] = across(eye, y_ref[:, at]).astype(bf16)
        return carry

    lax.fori_loop(0, 4, flip, 0)
    last = mats + 1

    def step(i, carry):
        @pl.when(i < 1)
        def _():
            permute(0)

        @pl.when(i < mats)
        def _():
            compute(i)

        @pl.when(i == 0)
        def _():
            pl.semaphore_wait(barrier, len(met) + 7)

        @pl.when(i < mats)
        def _():
            stage1(i)

        @pl.when((i >= 1) & (i < mats + 1))
        def _():
            stage2(i - 1)

        @pl.when(i == 0)
        def _():
            permute(1)

        @pl.when((i >= 1) & (i < 3))
        def _():
            permute(2 * i)
            permute(2 * i + 1)

        def small(*pairs):
            for at, work in pairs:
                @pl.when(i == at)
                def _(work=work):
                    work()

        def aux_start():
            aux_parts()
            stage1(aux, (1,))

        small((3, aux_start), (4, lambda: stage2(aux, (1,))), (5, aux_total), (6, aux_row))

        @pl.when((i >= 2) & (i < ringed + 2))
        def _():
            stage3(i - 2)

        @pl.when((i >= ringed + 2) & (i < mats + 2))
        def _():
            direct(i - 2)

        small((4, lambda: direct(aux, (1,))), (7, solve))

        @pl.when((i >= 3) & (i < ringed + 3))
        def _():
            stage4(i - 3)

        @pl.when((i >= 4) & (i < ringed + 4))
        def _():
            stage5(i - 4)

        return carry

    lax.fori_loop(0, mats + 2, step, 0)

    lane = iota((32, 128), 1)
    best = jnp.zeros((32, 128), f32)
    for m in range(perms):
        left, right = owned(m)
        peak = jnp.max(jnp.maximum(jnp.abs(left), jnp.abs(right)), axis=1, keepdims=True)
        best = jnp.where(lane == m, peak, best)
    pm[...] = best
    for d in range(1, 8):
        to_tile(pm, pmin.at[d - 1], 1, d).start()
    left, right = owned(own)
    obs_ref[:, :128] = left
    obs_ref[:, 128:] = right

    for h in range(2):
        all_of(in1.at[h, pl.ds(0, mats + h)], send1.at[h], recv1.at[0, 0, 0]).wait_send()
        all_of(in2.at[h], send2.at[h], recv2.at[0, 0, 0]).wait_send()
        all_of(inz.at[h], sendz.at[h], recvz.at[0, 0]).wait_send()
        all_of(ind.at[h, pl.ds(0, 2 + h)], sendd.at[h], recvd.at[0, 0]).wait_send()
    all_of(tt.at[pl.ds(0, 7)], sendx.at[0], recvx.at[0]).wait_send()
    all_of(agu.at[x, pl.ds(0, 7)], sendx.at[2], recvx.at[2]).wait_send()
    all_of(agu.at[pl.ds(0, 3)], sendx.at[3], recvx.at[3]).wait_send()
    all_of(pmin, sendx.at[1], recvx.at[1]).wait()
    for d in range(7):
        best = jnp.maximum(best, pmin[d])
    peak_ref[...] = best


def scan(traits, covariates, genotypes, shuffles, samples):
    perms = shuffles.shape[0]
    mats = perms + 1
    rows = traits.shape[0]
    vmem = pl.BlockSpec(memory_space=pltpu.VMEM)
    dma = pltpu.SemaphoreType.DMA
    return pl.pallas_call(
        functools.partial(scan_kernel, samples=samples),
        out_shape=(
            jax.ShapeDtypeStruct((32, 256), f32),
            jax.ShapeDtypeStruct((32, 128), f32),
        ),
        in_specs=[vmem] * 4,
        out_specs=(vmem, vmem),
        scratch_shapes=[
            pltpu.VMEM((1024, rows), bf16),
            pltpu.VMEM((mats, rows, 384), bf16),
            pltpu.VMEM((48, rows), bf16),
            pltpu.VMEM((32, 32, 128), f32),
            pltpu.VMEM((2, mats + 1, 4, 2, 4, 32, 128), f32),
            pltpu.VMEM((2, mats + 1, 6, 4, 32, 128), f32),
            pltpu.VMEM((2, mats + 1, 4, 2, 32, 128), f32),
            pltpu.VMEM((2, mats - 2, 6, 32, 128), f32),
            pltpu.VMEM((2, mats - 2, 2, 32, 128), f32),
            pltpu.VMEM((2, mats - 2, 32, 128), f32),
            pltpu.VMEM((2, 3, 7, 32, 128), f32),
            pltpu.VMEM((4, 8, 24, 128), f32),
            pltpu.VMEM((8, 8, 128), f32),
            pltpu.VMEM((mats * 72, 128), f32),
            pltpu.VMEM((128, mats * 256), f32),
            pltpu.VMEM((mats, 32, 256), f32),
            pltpu.VMEM((32, 128), f32),
            pltpu.VMEM((8, 256), f32),
            pltpu.VMEM((32, 128), f32),
            pltpu.VMEM((7, 32, 128), f32),
            dma((2,)), dma((2, mats + 1, 3)),
            dma((2,)), dma((2, mats - 2, 3)),
            dma((2,)), dma((2, mats - 2)),
            dma((2,)), dma((2, 3)),
            dma((4,)), dma((4,)),
        ],
        compiler_params=pltpu.CompilerParams(
            collective_id=0, has_side_effects=True, vmem_limit_bytes=56 * 1024 * 1024
        ),
    )(traits, covariates.T, genotypes, shuffles)


def shards(traits, covariates, genotypes, shuffles):
    samples = traits.shape[0] * lax.axis_size("samp")
    observed, peaks = scan(traits, covariates, genotypes, shuffles, samples)
    return (observed, peaks[:, : shuffles.shape[0]].T)


def solution(mesh):
    placed = (P("samp", None), P("samp", None), P("samp", "tile"), P(None, "samp"))
    return jax.shard_map(
        shards,
        mesh=mesh,
        in_specs=placed,
        out_specs=(P("samp", "tile"), P(None, "samp")),
        check_vma=False,
    )
```

time: 101 us -> 87.4 us (0.87)
  Pallas kernels: 96.1 us -> 83.8 us
  local copies, waits for them, and re-layouts: 4.43 us -> 2.76 us
    pallas_call x1, Pallas kernels: 96.1 us -> 83.8 us  [scan(): pl.pallas_call(functools.partial(scan_kernel, samples=samples), out_shape...]
    unnamed x3 -> x2, local copies, waits for them, and re-layouts: 3.71 us -> 2.04 us
where the time goes in v3:
time: 87.4 us; the launch traced here: 87.2 us
  Pallas kernels  83.8 us (96%)
  local copies, waits for them, and re-layouts  2.76 us (3%)
    pallas_call x1, Pallas kernels, scan(): pl.pallas_call(functools.partial(scan_kernel, samples=samples), out_shape...  83.8 us
    unnamed x2, local copies, waits for them, and re-layouts  2.04 us

profile of v3, /device:TPU:1, one launch (start us, length us, event | category | flops | bytes accessed | tf_op | source)
XLA Modules:
  0.0 87.2 jit_solution(11091791407237405999)
XLA Ops:
  0.6 83.8 %shard_map.59 = (f32[32,256]{1,0:T(8,128)}, f32[32,128]{1,0:T(8,128)}) custom-call(bf16[1024,1024]{1,0:T(8,128)(2,1)} %y_ref.1, bf16[32,1024]{1,0:T(8,128)(2,1)} %bitcast.3, s32[1024,256]{1,0:T(8,128)} %geno_ref.1, s32[6,1024]{1,0:T(8,128)} %order_ref.1), custom_call_target="tpu_custom_call" | custom-call | tf_op jit(solution)/shard_map/pallas_call | solution.py:469
  84.4 0.7 slice_bitcast_fusion
  85.1 0.7 copy.6
  85.8 1.4 %copy.8 = f32[32,256]{1,0:T(8,128)} copy(f32[32,256]{1,0:T(8,128)} %get-tuple-element.10) | data formatting | bytes 65536

commit v4 on v3

--- a/solution.py
+++ b/solution.py
@@ -17,6 +17,18 @@
 bf16 = jnp.bfloat16
 
 
+ORDER = (
+    "C1", "B", "11", "P3", "C3", "13", "P0", "C0", "211", "P5", "10", "P2",
+    "C2", "12", "231", "P4", "201", "200", "230", "aux", "A1", "210", "221", "220",
+    "C5", "311", "C4", "301", "A2", "310", "14", "C6", "331", "A3", "15", "410",
+    "321", "241", "411", "A4", "320", "251", "431", "240", "421", "250", "330", "16",
+    "341", "511", "A5", "340", "420", "521", "351", "401", "430", "260", "300", "441",
+    "531", "350", "440", "261", "A6", "501", "510", "400", "520", "450", "451", "541",
+    "540", "d61", "d60", "500", "550", "530", "551", "inv", "e60", "e61", "corr", "f3",
+    "f4", "f1", "f0", "f2", "f5", "T", "f6",
+)
+
+
 def exact_dot(a, b):
     return jnp.dot(a, b, preferred_element_type=f32, precision=lax.Precision.HIGHEST)
 
@@ -30,18 +42,19 @@
 
 
 def scan_kernel(
-    y_ref, cov_ref, geno_ref, order_ref, obs_ref, peak_ref,
-    yt, q, xt, tps, part, in1, mid, in2, low, inz, ind, agu, tt,
+    y_hbm, cov_hbm, geno_hbm, order_hbm, out_ref,
+    y_ref, cov_ref, geno_ref, order_ref, load,
+    yt, q, xt, tps, part, in1, mid, in2, low, inz, ind, lowin, agu, tt,
     lhs, vst, corr, st_ref, sg_ref, pm, pmin,
     send1, recv1, send2, recv2, sendz, recvz, sendd, recvd, sendx, recvx,
     *, samples,
 ):
-    perms = order_ref.shape[0]
+    perms = order_hbm.shape[0]
     mats = perms + 1
     own = perms
     aux = mats
-    ringed = perms - 1
-    rows = y_ref.shape[0]
+    ringed = perms - 0
+    rows = y_hbm.shape[0]
     s = lax.axis_index("samp")
     t = lax.axis_index("tile")
     x = lax.rem(s, 4)
@@ -51,24 +64,35 @@
     zl = t // 2
     base = s * rows
 
-    def at_x(d, dz=0):
-        return y * 8 + lax.rem(zh + dz, 2) * 4 + lax.rem(x + d, 4)
-
-    def at_y(d, dz=0):
-        return lax.rem(y + d, 4) * 8 + lax.rem(zh + dz, 2) * 4 + x
+    def at_x(d):
+        return s - x + lax.rem(x + d, 4)
+
+    def at_y(d):
+        return lax.rem(s + 8 * d, 32)
+
+    z_peer = s + 4 - 8 * zh
 
     place = (x, y)
     along = (at_x, at_y)
-    apart = [(d, dz) for d in range(4) for dz in range(2) if d or dz]
 
     barrier = pltpu.get_barrier_semaphore()
-    met = [at_y(d, dz) for d, dz in apart] + [at_x(d, dz) for d, dz in apart if d]
+    met = [at_y(d) for d in (1, 2, 3)] + [at_x(d) for d in (1, 2, 3)] + [z_peer]
     for peer in met:
         pl.semaphore_signal(barrier, inc=1, device_id={"samp": peer}, device_id_type=MESH)
     for d in range(1, 8):
         pl.semaphore_signal(
             barrier, inc=1, device_id={"tile": lax.rem(t + d, 8)}, device_id_type=MESH
         )
+
+    loads = [
+        pltpu.make_async_copy(a, b, load.at[k])
+        for k, (a, b) in enumerate(
+            [(cov_hbm, cov_ref), (geno_hbm, geno_ref), (order_hbm, order_ref)]
+            + [(y_hbm.at[:, pl.ds(k, 256)], y_ref.at[:, pl.ds(k, 256)]) for k in range(0, 1024, 256)]
+        )
+    ]
+    for copy in loads:
+        copy.start()
 
     def remote(src, dst, send, recv, peer):
         return pltpu.make_async_remote_copy(
@@ -102,7 +126,7 @@
 
     def z_copy(h, m):
         return remote(
-            low.at[h, m, 1 - zh], inz.at[h, m], sendz.at[h], recvz.at[h, m], at_x(0, 1)
+            low.at[h, m, 1 - zh], inz.at[h, m], sendz.at[h], recvz.at[h, m], z_peer
         )
 
     def compute(m):
@@ -149,22 +173,22 @@
         mid[h, m, :, 0] = part[h, m, c, 0] + in1[h, m, 3] + in1[h, m, 4]
         mid[h, m, :, 1] = part[h, m, c, 1] + in1[h, m, 2] + in1[h, m, 5]
 
-    def stage3(m):
-        for h in range(2):
+    def stage3(m, halves=(0, 1)):
+        for h in halves:
             first_sum(h, m)
             for k in range(4):
                 second_copy(h, m, k).start()
 
-    def stage4(m):
-        for h in range(2):
+    def stage4(m, halves=(0, 1)):
+        for h in halves:
             c = place[1 - h]
             for k, d, uv in ((0, 1, 0), (1, 3, 1)):
                 second_copy(h, m, k).wait_recv()
                 in2[h, m, k] = in2[h, m, k] + mid[h, m, lax.rem(c + d, 4), uv]
                 second_copy(h, m, k + 4).start()
 
-    def stage5(m):
-        for h in range(2):
+    def stage5(m, halves=(0, 1)):
+        for h in halves:
             c = place[1 - h]
             all_of(in2.at[h, m, pl.ds(2, 4)], send2.at[h], recv2.at[h, m, 2]).wait_recv()
             low[h, m, 0] = mid[h, m, c, 0] + in2[h, m, 3] + in2[h, m, 4]
@@ -175,20 +199,21 @@
     def direct(m, halves=(0, 1)):
         for h in halves:
             first_sum(h, m)
-            for k, (d, dz) in enumerate(apart):
-                blk = lax.rem(place[1 - h] + d, 4)
+            for d in (1, 3, 2):
                 remote(
-                    mid.at[h, m, blk, lax.rem(zh + dz, 2)], ind.at[h, m - ringed, k],
-                    sendd.at[h], recvd.at[h, m - ringed], along[1 - h](d, dz),
+                    mid.at[h, m, lax.rem(place[1 - h] + d, 4)], ind.at[h, m - ringed, d - 1],
+                    sendd.at[h], recvd.at[h, m - ringed], along[1 - h](d),
                 ).start()
 
     def direct_sum(h, m):
         n = m - ringed
         all_of(ind.at[h, n], sendd.at[h], recvd.at[h, n]).wait_recv()
-        total = mid[h, m, place[1 - h], zh]
-        for k in range(7):
-            total = total + ind[h, n, k]
-        return total
+        low[h, m] = mid[h, m, place[1 - h]] + ind[h, n, 0] + ind[h, n, 1] + ind[h, n, 2]
+
+    def stage5d(m, halves=(0, 1)):
+        for h in halves:
+            direct_sum(h, m)
+            z_copy(h, m).start()
 
 
     def aux_parts():
@@ -237,18 +262,25 @@
         mine = tps[:, pl.ds(pl.multiple_of(zl * 8, 8), 8), :]
         part[1, aux, :, :, :, 0:8] = mine.reshape(4, 2, 4, 8, 128)
 
+    def both_copy():
+        return remote(low.at[1, aux], lowin, sendx.at[4], recvx.at[4], z_peer)
+
+    def aux_low():
+        direct_sum(1, aux)
+        both_copy().start()
+
     def aux_total():
-        total = direct_sum(1, aux)
-        agu[x, y * 2 + zh] = total[8:]
-        tt[t] = total[:8]
-        for d, dz in apart:
-            ref = agu.at[x, y * 2 + zh]
-            remote(ref, ref, sendx.at[2], recvx.at[2], at_y(d, dz)).start()
+        both_copy().wait_recv()
+        total = low[1, aux] + lowin[...]
+        agu[x, y] = total[:, 8:]
+        for d in (1, 3, 2):
+            remote(agu.at[x, y], agu.at[x, y], sendx.at[2], recvx.at[2], at_y(d)).start()
+        tt[t] = jnp.where(zh == 0, total[0, :8], total[1, :8])
         for d in range(1, 8):
             to_tile(tt.at[t], tt.at[t], 0, d).start()
 
     def aux_row():
-        all_of(agu.at[x, pl.ds(0, 7)], sendx.at[2], recvx.at[2]).wait_recv()
+        all_of(agu.at[x, pl.ds(0, 3)], sendx.at[2], recvx.at[2]).wait_recv()
         for d in (1, 3, 2):
             remote(agu.at[x], agu.at[x], sendx.at[3], recvx.at[3], at_x(d)).start()
 
@@ -261,10 +293,10 @@
         row8 = iota((8, 128), 0)
 
         def eight(k):
-            return agu[0, 7, 8 * k : 8 * k + 8]
+            return agu[0, 3, 1, 8 * k : 8 * k + 8]
 
         def product(m, k):
-            return agu[:, m, 8 * k : 8 * k + 8].reshape(32, 128)
+            return agu[:, m // 2, m % 2, 8 * k : 8 * k + 8].reshape(32, 128)
 
         sums = eight(2)[0:1]
         sum_column = jnp.sum(jnp.where(lane == row, sums, 0.0), axis=1, keepdims=True)
@@ -305,6 +337,9 @@
             column = inv[:, k : k + 1]
             rest = jnp.where(lane40 == k, 0.0, inv)
             inv = jnp.where(row40 == k, line, rest - column * line)
+        return inv, gram, gram_of, geno_of, trait_of, ones_g, squares_y
+
+    def corrections(inv, gram, gram_of, geno_of, trait_of, ones_g, squares_y):
         pad128 = jnp.zeros((88, 128), f32)
         pad256 = jnp.zeros((88, 256), f32)
         geno0 = geno_of(own)
@@ -340,15 +375,14 @@
     def owned(m):
         outs = []
         for h in range(2):
-            if m < ringed:
-                z_copy(h, m).wait_recv()
-                total = low[h, m, zh] + inz[h, m]
-            else:
-                total = direct_sum(h, m)
+            z_copy(h, m).wait_recv()
+            total = low[h, m, zh] + inz[h, m]
             cols = slice(h * 128, h * 128 + 128)
             outs.append((total - corr[m, :, cols]) * st_ref[...] * sg_ref[0:1, cols])
         return outs
 
+    loads[0].wait()
+    loads[1].wait()
     spread = jnp.where(lax.rem(iota((32, 128), 1), 32) == iota((32, 128), 0), 1.0, 0.0)
     spread = spread.astype(bf16)
     for b in range(4):
@@ -361,120 +395,92 @@
     xt[32:] = jnp.where(iota((16, rows), 0) == 0, 1.0, 0.0).astype(bf16)
     eye = jnp.where(iota((256, 256), 0) == iota((256, 256), 1), 1.0, 0.0).astype(bf16)
 
-    def flip(b, carry):
-        at = pl.ds(pl.multiple_of(b * 256, 256), 256)
+    loads[2].wait()
+    permute(1)
+    for b in range(4):
+        loads[3 + b].wait()
+        at = slice(b * 256, b * 256 + 256)
         yt[at, :] = across(eye, y_ref[:, at]).astype(bf16)
-        return carry
-
-    lax.fori_loop(0, 4, flip, 0)
-    last = mats + 1
-
-    def step(i, carry):
-        @pl.when(i < 1)
-        def _():
-            permute(0)
-
-        @pl.when(i < mats)
-        def _():
-            compute(i)
-
-        @pl.when(i == 0)
-        def _():
-            pl.semaphore_wait(barrier, len(met) + 7)
-
-        @pl.when(i < mats)
-        def _():
-            stage1(i)
-
-        @pl.when((i >= 1) & (i < mats + 1))
-        def _():
-            stage2(i - 1)
-
-        @pl.when(i == 0)
-        def _():
-            permute(1)
-
-        @pl.when((i >= 1) & (i < 3))
-        def _():
-            permute(2 * i)
-            permute(2 * i + 1)
-
-        def small(*pairs):
-            for at, work in pairs:
-                @pl.when(i == at)
-                def _(work=work):
-                    work()
-
-        def aux_start():
-            aux_parts()
-            stage1(aux, (1,))
-
-        small((3, aux_start), (4, lambda: stage2(aux, (1,))), (5, aux_total), (6, aux_row))
-
-        @pl.when((i >= 2) & (i < ringed + 2))
-        def _():
-            stage3(i - 2)
-
-        @pl.when((i >= ringed + 2) & (i < mats + 2))
-        def _():
-            direct(i - 2)
-
-        small((4, lambda: direct(aux, (1,))), (7, solve))
-
-        @pl.when((i >= 3) & (i < ringed + 3))
-        def _():
-            stage4(i - 3)
-
-        @pl.when((i >= 4) & (i < ringed + 4))
-        def _():
-            stage5(i - 4)
-
-        return carry
-
-    lax.fori_loop(0, mats + 2, step, 0)
 
     lane = iota((32, 128), 1)
-    best = jnp.zeros((32, 128), f32)
-    for m in range(perms):
+    held = {"best": jnp.zeros((32, 128), f32)}
+
+    def finish(m):
         left, right = owned(m)
+        if m == own:
+            out_ref[:32, :128] = left
+            out_ref[:32, 128:] = right
+            out_ref[32:, 128:] = jnp.zeros((8, 128), f32)
+            return
         peak = jnp.max(jnp.maximum(jnp.abs(left), jnp.abs(right)), axis=1, keepdims=True)
-        best = jnp.where(lane == m, peak, best)
-    pm[...] = best
-    for d in range(1, 8):
-        to_tile(pm, pmin.at[d - 1], 1, d).start()
-    left, right = owned(own)
-    obs_ref[:, :128] = left
-    obs_ref[:, 128:] = right
+        held["best"] = jnp.where(lane == m, peak, held["best"])
+
+    def exchange():
+        pm[...] = held["best"]
+        for d in range(1, 8):
+            to_tile(pm, pmin.at[d - 1], 1, d).start()
+
+    def invert():
+        held["solved"] = solve()
+
+    stages = {"2": stage2, "3": stage3, "4": stage4, "5": stage5, "d": direct, "e": stage5d}
+    whole = {"P": permute, "C": compute, "1": stage1, "f": finish}
+    single = {
+        "aux": aux_parts,
+        "A1": lambda: stage1(aux, (1,)),
+        "A2": lambda: stage2(aux, (1,)),
+        "A3": lambda: direct(aux, (1,)),
+        "A4": aux_low,
+        "A5": aux_total,
+        "A6": aux_row,
+        "inv": invert,
+        "corr": lambda: corrections(*held["solved"]),
+        "T": exchange,
+        "B": lambda: pl.semaphore_wait(barrier, len(met) + 7),
+    }
+    for name in ORDER:
+        if name in single:
+            single[name]()
+        elif name[0] in whole:
+            whole[name[0]](int(name[1]))
+        else:
+            stages[name[0]](int(name[1]), (int(name[2]),))
+    best = held["best"]
 
     for h in range(2):
         all_of(in1.at[h, pl.ds(0, mats + h)], send1.at[h], recv1.at[0, 0, 0]).wait_send()
         all_of(in2.at[h], send2.at[h], recv2.at[0, 0, 0]).wait_send()
         all_of(inz.at[h], sendz.at[h], recvz.at[0, 0]).wait_send()
-        all_of(ind.at[h, pl.ds(0, 2 + h)], sendd.at[h], recvd.at[0, 0]).wait_send()
+        all_of(ind.at[h, pl.ds(0, mats - ringed + h)], sendd.at[h], recvd.at[0, 0]).wait_send()
     all_of(tt.at[pl.ds(0, 7)], sendx.at[0], recvx.at[0]).wait_send()
-    all_of(agu.at[x, pl.ds(0, 7)], sendx.at[2], recvx.at[2]).wait_send()
+    all_of(agu.at[x, pl.ds(0, 3)], sendx.at[2], recvx.at[2]).wait_send()
+    both_copy().wait_send()
     all_of(agu.at[pl.ds(0, 3)], sendx.at[3], recvx.at[3]).wait_send()
     all_of(pmin, sendx.at[1], recvx.at[1]).wait()
     for d in range(7):
         best = jnp.maximum(best, pmin[d])
-    peak_ref[...] = best
+    best = jnp.concatenate([best, jnp.zeros((96, 128), f32)], axis=0)
+    out_ref[32:, :128] = jnp.transpose(best)[:8]
 
 
 def scan(traits, covariates, genotypes, shuffles, samples):
     perms = shuffles.shape[0]
     mats = perms + 1
+    ringed = perms - 0
     rows = traits.shape[0]
     vmem = pl.BlockSpec(memory_space=pltpu.VMEM)
     dma = pltpu.SemaphoreType.DMA
     return pl.pallas_call(
         functools.partial(scan_kernel, samples=samples),
-        out_shape=(
-            jax.ShapeDtypeStruct((32, 256), f32),
-            jax.ShapeDtypeStruct((32, 128), f32),
-        ),
-        in_specs=[vmem] * 4,
-        out_specs=(vmem, vmem),
+        out_shape=jax.ShapeDtypeStruct((40, 256), f32),
+        in_specs=[pl.BlockSpec(memory_space=pl.ANY)] * 4,
+        out_specs=vmem,
         scratch_shapes=[
+            pltpu.VMEM(traits.shape, bf16),
+            pltpu.VMEM(covariates.shape[::-1], bf16),
+            pltpu.VMEM(genotypes.shape, jnp.int32),
+            pltpu.VMEM(shuffles.shape, jnp.int32),
+            dma((7,)),
             pltpu.VMEM((1024, rows), bf16),
             pltpu.VMEM((mats, rows, 384), bf16),
             pltpu.VMEM((48, rows), bf16),
@@ -482,11 +488,12 @@
             pltpu.VMEM((2, mats + 1, 4, 2, 4, 32, 128), f32),
             pltpu.VMEM((2, mats + 1, 6, 4, 32, 128), f32),
             pltpu.VMEM((2, mats + 1, 4, 2, 32, 128), f32),
-            pltpu.VMEM((2, mats - 2, 6, 32, 128), f32),
-            pltpu.VMEM((2, mats - 2, 2, 32, 128), f32),
-            pltpu.VMEM((2, mats - 2, 32, 128), f32),
-            pltpu.VMEM((2, 3, 7, 32, 128), f32),
-            pltpu.VMEM((4, 8, 24, 128), f32),
+            pltpu.VMEM((2, ringed, 6, 32, 128), f32),
+            pltpu.VMEM((2, mats + 1, 2, 32, 128), f32),
+            pltpu.VMEM((2, mats, 32, 128), f32),
+            pltpu.VMEM((2, mats + 1 - ringed, 3, 2, 32, 128), f32),
+            pltpu.VMEM((2, 32, 128), f32),
+            pltpu.VMEM((4, 4, 2, 24, 128), f32),
             pltpu.VMEM((8, 8, 128), f32),
             pltpu.VMEM((mats * 72, 128), f32),
             pltpu.VMEM((128, mats * 256), f32),
@@ -496,10 +503,10 @@
             pltpu.VMEM((32, 128), f32),
             pltpu.VMEM((7, 32, 128), f32),
             dma((2,)), dma((2, mats + 1, 3)),
-            dma((2,)), dma((2, mats - 2, 3)),
-            dma((2,)), dma((2, mats - 2)),
-            dma((2,)), dma((2, 3)),
-            dma((4,)), dma((4,)),
+            dma((2,)), dma((2, ringed, 3)),
+            dma((2,)), dma((2, mats)),
+            dma((2,)), dma((2, mats + 1 - ringed)),
+            dma((5,)), dma((5,)),
         ],
         compiler_params=pltpu.CompilerParams(
             collective_id=0, has_side_effects=True, vmem_limit_bytes=56 * 1024 * 1024
@@ -509,8 +516,8 @@
 
 def shards(traits, covariates, genotypes, shuffles):
     samples = traits.shape[0] * lax.axis_size("samp")
-    observed, peaks = scan(traits, covariates, genotypes, shuffles, samples)
-    return (observed, peaks[:, : shuffles.shape[0]].T)
+    out = scan(traits, covariates, genotypes, shuffles, samples)
+    return (out[:32], out[32 : 32 + shuffles.shape[0], :32])
 
 
 def solution(mesh):

time: 87.4 us -> 75.4 us (0.86)
  Pallas kernels: 83.8 us -> 71.9 us
    pallas_call x1, Pallas kernels: 83.8 us -> 71.9 us  [scan(): pl.pallas_call(functools.partial(scan_kernel, samples=samples), out_shape...]
    slice x0 -> x2, local copies, waits for them, and re-layouts: none -> 2.64 us  [shards(): return (out[:32], out[32:32 + shuffles.shape[0], :32])]
    unnamed x2 -> x0, local copies, waits for them, and re-layouts: 2.04 us -> none
where the time goes in v4:
time: 75.4 us; the launch traced here: 75.2 us
  Pallas kernels  71.9 us (95%)
  local copies, waits for them, and re-layouts  2.64 us (4%)
    pallas_call x1, Pallas kernels, scan(): pl.pallas_call(functools.partial(scan_kernel, samples=samples), out_shape...  71.9 us
    slice x2, local copies, waits for them, and re-layouts, shards(): return (out[:32], out[32:32 + shuffles.shape[0], :32])  2.64 us

profile of v4, /device:TPU:1, one launch (start us, length us, event | category | flops | bytes accessed | tf_op | source)
XLA Modules:
  0.0 75.2 jit_solution(8625853640343726650)
XLA Ops:
  0.6 71.9 %shard_map.59 = f32[40,256]{1,0:T(8,128)} custom-call(bf16[1024,1024]{1,0:T(8,128)(2,1)} %y_hbm.1, bf16[32,1024]{1,0:T(8,128)(2,1)} %bitcast.1, s32[1024,256]{1,0:T(8,128)} %geno_hbm.1, s32[6,1024]{1,0:T(8,128)} %order_hbm.1), custom_call_target="tpu_custom_call" | custom-call | tf_op jit(solution)/shard_map/pallas_call | solution.py:473
  72.6 1.3 %slice.7 = f32[6,32]{1,0:T(8,128)} slice(f32[40,256]{1,0:T(8,128)} %shard_map.59), slice={[32:38], [0:32]} | slice | bytes 1536 | tf_op jit(solution)/shard_map/slice | solution.py:520
  73.8 1.4 %slice.6 = f32[32,256]{1,0:T(8,128)} slice(f32[40,256]{1,0:T(8,128)} %shard_map.59), slice={[0:32], [0:256]} | slice | bytes 65536 | tf_op jit(solution)/shard_map/slice | solution.py:520

commit v5 on v4

v5 whole, which is shorter than its diff:
```python
import functools
import math

import jax
import jax.numpy as jnp
from jax import lax
from jax.experimental import pallas as pl
from jax.experimental.pallas import tpu as pltpu
from jax.sharding import PartitionSpec as P

C = 32


epsilon = 1e-05
MESH = pl.DeviceIdType.MESH
f32 = jnp.float32
bf16 = jnp.bfloat16


ORDER = (
    "C0", "B", "10", "P1", "C1", "11", "P3", "g1", "P2", "200", "C3", "13",
    "P5", "C2", "P4", "12", "aux", "A1", "210", "C5", "g2", "201", "220", "A2",
    "221", "C4", "211", "15", "231", "A3", "250", "230", "310", "321", "311", "C6",
    "A4", "14", "320", "301", "300", "g3", "331", "330", "410", "241", "421", "240",
    "251", "411", "A5", "400", "401", "16", "inv", "341", "431", "430", "420", "d51",
    "510", "260", "521", "340", "501", "441", "500", "d50", "261", "A6", "531", "530",
    "511", "440", "520", "d60", "e51", "541", "ct", "e50", "d61", "540", "corr", "f1",
    "f0", "f2", "e60", "e61", "f5", "f4", "f3", "T", "f6",
)


def exact_dot(a, b):
    return jnp.dot(a, b, preferred_element_type=f32, precision=lax.Precision.HIGHEST)


def split(a):
    high = a.astype(bf16)
    rest = a - high.astype(f32)
    middle = rest.astype(bf16)
    return high, middle, (rest - middle.astype(f32)).astype(bf16)


def across(a, b):
    return lax.dot_general(a, b, (((1,), (1,)), ((), ())), preferred_element_type=f32)


def iota(shape, dim):
    return lax.broadcasted_iota(jnp.int32, shape, dim)


def scan_kernel(
    y_hbm, cov_hbm, geno_hbm, order_hbm, out_ref,
    y_ref, cov_ref, geno_ref, order_ref, load,
    yt, q, xt, tps, part, in1, mid, in2, low, inz, ind,
    apart, ain1, amid, aind, alow, alowin, agu, tt, gsum, gin,
    inv_ref, ct_ref, lhs, vst, corr, st_ref, sg_ref, pm, pmin,
    send1, recv1, send2, recv2, sendz, recvz, sendd, recvd, sendx, recvx,
    *, samples,
):
    perms = order_hbm.shape[0]
    mats = perms + 1
    own = perms
    aux = mats
    ringed = perms - 1
    rows = y_hbm.shape[0]
    s = lax.axis_index("samp")
    t = lax.axis_index("tile")
    x = lax.rem(s, 4)
    zh = lax.rem(s // 4, 2)
    y = s // 8
    core = lax.rem(t, 2)
    zl = t // 2
    base = s * rows

    def at_x(d):
        return s - x + lax.rem(x + d, 4)

    def at_y(d):
        return lax.rem(s + 8 * d, 32)

    z_peer = s + 4 - 8 * zh

    place = (x, y)
    along = (at_x, at_y)

    barrier = pltpu.get_barrier_semaphore()
    met = [at_y(d) for d in (1, 2, 3)] + [at_x(d) for d in (1, 2, 3)] + [z_peer]
    for peer in met:
        pl.semaphore_signal(barrier, inc=1, device_id={"samp": peer}, device_id_type=MESH)
    for d in range(1, 8):
        pl.semaphore_signal(
            barrier, inc=1, device_id={"tile": lax.rem(t + d, 8)}, device_id_type=MESH
        )

    loads = [
        pltpu.make_async_copy(a, b, load.at[k])
        for k, (a, b) in enumerate(
            [(cov_hbm, cov_ref), (geno_hbm, geno_ref), (order_hbm, order_ref)]
            + [(y_hbm.at[:, pl.ds(k, 256)], y_ref.at[:, pl.ds(k, 256)]) for k in range(0, 1024, 256)]
        )
    ]
    for copy in loads:
        copy.start()

    def remote(src, dst, send, recv, peer):
        return pltpu.make_async_remote_copy(
            src_ref=src, dst_ref=dst, send_sem=send, recv_sem=recv,
            device_id={"samp": peer}, device_id_type=MESH,
        )

    def to_tile(src, dst, k, d):
        return pltpu.make_async_remote_copy(
            src_ref=src, dst_ref=dst, send_sem=sendx.at[k], recv_sem=recvx.at[k],
            device_id={"tile": lax.rem(t + d, 8)}, device_id_type=MESH,
        )

    def all_of(ref, send, recv):
        return remote(ref, ref, send, recv, at_x(1))

    def ring_copy(src, buf, k, c, peers, send, recv):
        blk = lax.rem(c + (2, 2, 1, 3, 1, 3)[k], 4)
        uv = (0, 1, 1, 0, 0, 1)[k]
        ref = buf.at[k - 4] if k >= 4 else src.at[blk, uv]
        return remote(ref, buf.at[k], send, recv.at[min(k, 2)], peers((1, 3, 1, 3, 1, 3)[k]))

    def part_of(h, m):
        return apart if m == aux else part.at[h, m]

    def in1_of(h, m):
        return ain1 if m == aux else in1.at[h, m]

    def mid_of(h, m):
        return amid if m == aux else mid.at[h, m]

    def ind_of(h, m):
        return aind if m == aux else ind.at[h, m - ringed]

    def low_of(h, m):
        return alow if m == aux else low.at[h, m]

    def first_copy(h, m, k):
        return ring_copy(
            part_of(h, m), in1_of(h, m), k, place[h], along[h],
            send1.at[2 if m == aux else h], recv1.at[h, m],
        )

    def second_copy(h, m, k):
        return ring_copy(
            mid.at[h, m], in2.at[h, m], k, place[1 - h], along[1 - h], send2.at[h],
            recv2.at[h, m],
        )

    def z_copy(h, m):
        return remote(
            low.at[h, m, 1 - zh], inz.at[h, m], sendz.at[h], recvz.at[h, m], z_peer
        )

    def compute(m):
        out = jnp.dot(yt[...], q[m, :, :256], preferred_element_type=f32)
        for o in range(32):
            yb, z, xb = o // 8, o // 4 % 2, o % 4
            piece = out[o * 32 : o * 32 + 32]
            part[0, m, xb, z, yb] = piece[:, :128]
            part[1, m, yb, z, xb] = piece[:, 128:]

    def permute(m):
        order = order_ref[pl.ds(m, 1), :] - base
        hot = jnp.where(iota((rows, rows), 0) == order, 1.0, 0.0).astype(bf16)
        q[m] = jnp.dot(hot, q[own], preferred_element_type=f32).astype(bf16)

    def stage1(m, halves=(0, 1)):
        for k in range(4):
            for h in halves:
                first_copy(h, m, k).start()

    def stage2(m, halves=(0, 1)):
        for h in halves:
            c = place[h]
            lines, buf = part_of(h, m), in1_of(h, m)
            for k, d, uv in ((0, 1, 0), (1, 3, 1)):
                first_copy(h, m, k).wait_recv()
                buf[k] = buf[k] + lines[lax.rem(c + d, 4), uv]
                first_copy(h, m, k + 4).start()

    def first_sum(h, m):
        c = place[h]
        lines, buf, to = part_of(h, m), in1_of(h, m), mid_of(h, m)
        all_of(buf.at[pl.ds(2, 4)], send1.at[h], recv1.at[h, m, 2]).wait_recv()
        to[:, 0] = lines[c, 0] + buf[3] + buf[4]
        to[:, 1] = lines[c, 1] + buf[2] + buf[5]

    def stage3(m, halves=(0, 1)):
        for h in halves:
            first_sum(h, m)
            for k in range(4):
                second_copy(h, m, k).start()

    def stage4(m, halves=(0, 1)):
        for h in halves:
            c = place[1 - h]
            for k, d, uv in ((0, 1, 0), (1, 3, 1)):
                second_copy(h, m, k).wait_recv()
                in2[h, m, k] = in2[h, m, k] + mid[h, m, lax.rem(c + d, 4), uv]
                second_copy(h, m, k + 4).start()

    def stage5(m, halves=(0, 1)):
        for h in halves:
            c = place[1 - h]
            all_of(in2.at[h, m, pl.ds(2, 4)], send2.at[h], recv2.at[h, m, 2]).wait_recv()
            low[h, m, 0] = mid[h, m, c, 0] + in2[h, m, 3] + in2[h, m, 4]
            low[h, m, 1] = mid[h, m, c, 1] + in2[h, m, 2] + in2[h, m, 5]
            z_copy(h, m).start()


    def direct(m, halves=(0, 1)):
        for h in halves:
            first_sum(h, m)
            for d in (1, 3, 2):
                remote(
                    mid_of(h, m).at[lax.rem(place[1 - h] + d, 4)], ind_of(h, m).at[d - 1],
                    sendd.at[2 if m == aux else h], recvd.at[h, m - ringed], along[1 - h](d),
                ).start()

    def direct_sum(h, m):
        buf = ind_of(h, m)
        all_of(buf, sendd.at[h], recvd.at[h, m - ringed]).wait_recv()
        total = mid_of(h, m)[place[1 - h]] + buf[0] + buf[1] + buf[2]
        low_of(h, m)[...] = total

    def stage5d(m, halves=(0, 1)):
        for h in halves:
            direct_sum(h, m)
            z_copy(h, m).start()


    def spread_of(m):
        return q[m, :, 256:].astype(f32)

    def aux_parts():
        for m in range(mats):
            out = jnp.dot(xt[...], q[m, :, :256], preferred_element_type=f32)
            for j in range(4):
                for k in range(2):
                    apart[m // 2, m % 2, j, 8 + 8 * k : 16 + 8 * k] = out[
                        8 * j : 8 * j + 8, 128 * k : 128 * k + 128
                    ]
        group = iota((rows, 128), 1) // 32
        picked = []
        for k in range(2):
            value = spread_of(3) if k == 0 else jnp.where(
                iota((rows, 128), 1) == 96, 1.0, 0.0
            )
            for j in range(3):
                value = jnp.where(group == j, spread_of(4 * k + j), value)
            picked.append(value)
            out = jnp.dot(xt[...], value.astype(bf16), preferred_element_type=f32)
            for j in range(4):
                apart[3, 1, j, 8 + 8 * k : 16 + 8 * k] = out[8 * j : 8 * j + 8]
        mine = jnp.where(core == 0, picked[0], picked[1]).astype(bf16)
        out = jnp.dot(yt[...], mine, preferred_element_type=f32)
        wide = yt[...].astype(f32)
        square_at = (iota((1024, 128), 1) == 97) & (core == 1)
        out = jnp.where(square_at, jnp.sum(wide * wide, axis=1, keepdims=True), out)
        tps[...] = out.reshape(32, 32, 128)
        ours = tps[:, pl.ds(pl.multiple_of(zl * 8, 8), 8), :]
        apart[:, :, :, 0:8] = ours.reshape(4, 2, 4, 8, 128)

    def both_copy():
        return remote(alow, alowin, sendx.at[4], recvx.at[4], z_peer)

    def aux_low():
        direct_sum(1, aux)
        both_copy().start()

    def aux_total():
        both_copy().wait_recv()
        total = alow[...] + alowin[...]
        agu[x, y] = total[:, 8:]
        for d in (1, 3, 2):
            remote(agu.at[x, y], agu.at[x, y], sendx.at[2], recvx.at[2], at_y(d)).start()
        tt[t] = jnp.where(zh == 0, total[0, :8], total[1, :8])
        for d in range(1, 8):
            to_tile(tt.at[t], tt.at[t], 0, d).start()

    def aux_row():
        all_of(agu.at[x, pl.ds(0, 3)], sendx.at[2], recvx.at[2]).wait_recv()
        for d in (1, 3, 2):
            remote(agu.at[x], agu.at[x], sendx.at[3], recvx.at[3], at_x(d)).start()


    def gram_send(n):
        for d in (1, 3, 2) if n < 2 else (0,):
            peer = z_peer if n == 2 else along[n](d)
            remote(
                gsum.at[n], gin.at[3 * n + max(d - 1, 0)], sendx.at[5 + n], recvx.at[5 + n], peer
            ).start()

    def gram_start():
        lane = iota((rows, 128), 1)
        wide = jnp.where(lane < 32, spread_of(own), jnp.where(lane == 32, 1.0, 0.0))
        out = jnp.dot(xt[...], wide.astype(bf16), preferred_element_type=f32)[:40]
        geno = q[own, :, :256].astype(f32)
        row = iota((40, 128), 0)
        for k in range(2):
            half = geno[:, 128 * k : 128 * k + 128]
            out = jnp.where(row == 33 + k, jnp.sum(half, axis=0, keepdims=True), out)
            out = jnp.where(row == 35 + k, jnp.sum(half * half, axis=0, keepdims=True), out)
        gsum[0] = out
        gram_send(0)

    def gram_pass(n):
        count = 1 if n == 3 else 3
        at = 3 * n - 3
        all_of(gin.at[pl.ds(at, count)], sendx.at[4 + n], recvx.at[4 + n]).wait_recv()
        total = gsum[n - 1]
        for k in range(count):
            total = total + gin[at + k]
        gsum[n] = total
        if n < 3:
            gram_send(n)

    def invert():
        gram_pass(3)
        lane40 = iota((40, 128), 1)
        row40 = iota((40, 128), 0)
        inv = jnp.where(row40 < C + 1, gsum[3], 0.0)
        for k in range(C + 1):
            pivot = inv[k : k + 1, k : k + 1]
            line = jnp.where(lane40[:1] == k, 1.0, inv[k : k + 1, :]) / pivot
            column = inv[:, k : k + 1]
            rest = jnp.where(lane40 == k, 0.0, inv)
            inv = jnp.where(row40 == k, line, rest - column * line)
        inv_ref[:40] = inv
        inv_ref[40:] = jnp.zeros((88, 128), f32)

    def trait_side():
        all_of(tt.at[pl.ds(0, 7)], sendx.at[0], recvx.at[0]).wait_recv()
        lane = iota((32, 128), 1)
        sums = [jnp.concatenate([tt[2 * k + c] for k in range(4)], axis=0) for c in range(2)]
        ones_y = sums[1][:, 96:97]
        squares_y = sums[1][:, 97:98]
        for m in range(mats):
            mine = sums[m // 4]
            k = m % 4
            if k:
                mine = pltpu.roll(mine, 128 - 32 * k, 1)
            mine = jnp.where(lane < 32, mine, jnp.where(lane == 32, ones_y, 0.0))
            lhs[mats * 40 + m * 32 : mats * 40 + m * 32 + 32] = mine
        coef_t = exact_dot(mine, inv_ref[...])
        coef_t = coef_t.astype(bf16).astype(f32)
        ct_ref[...] = coef_t
        gram = jnp.where(iota((40, 128), 0) < C + 1, gsum[3], 0.0)
        back = exact_dot(coef_t, jnp.concatenate([gram, jnp.zeros((88, 128), f32)], axis=0))
        squares_t = squares_y - jnp.sum(coef_t * (2.0 * mine - back), axis=1, keepdims=True)
        mean_t = jnp.maximum(squares_t, 0.0) / samples
        factor_z = math.sqrt(samples - C - 2) / samples
        st_ref[...] = jnp.broadcast_to(lax.rsqrt(mean_t + epsilon) * factor_z, (32, 128))

    def corrections():
        all_of(agu.at[pl.ds(0, 3)], sendx.at[3], recvx.at[3]).wait_recv()
        lane = iota((32, 128), 1)

        def product(m, k):
            return agu[:, m // 2, m % 2, 8 * k : 8 * k + 8].reshape(32, 128)

        gram = gsum[3]
        first = iota((8, 128), 0) == 0
        last_rows = jnp.where(first, gram[32:40], 0.0)
        ones_g = jnp.concatenate([gram[33:34], gram[34:35]], axis=1)
        squares_g = jnp.concatenate([gram[35:36], gram[36:37]], axis=1)
        ones_rows = jnp.where(iota((8, 256), 0) == 0, ones_g, 0.0)
        spreads = [product(7, 0), product(7, 1)]

        def geno_of(m):
            body = jnp.concatenate([product(m, 0), product(m, 1)], axis=1)
            return jnp.concatenate([body, ones_rows], axis=0)

        for m in range(mats):
            if m == own:
                body = gram[:32]
            else:
                body = spreads[m // 4]
                if m % 4:
                    body = pltpu.roll(body, 128 - 32 * (m % 4), 1)
                body = jnp.where(lane < 32, body, jnp.where(lane == 32, gram[:32], 0.0))
            lhs[m * 40 : m * 40 + 32] = body
            lhs[m * 40 + 32 : m * 40 + 40] = last_rows
        geno0 = geno_of(own)
        pad256 = jnp.zeros((88, 256), f32)
        coef_g = exact_dot(inv_ref[:40], jnp.concatenate([geno0, pad256], axis=0))
        rounded_g = jnp.concatenate([coef_g, pad256], axis=0).astype(bf16)
        coef_g = coef_g.astype(bf16).astype(f32)
        rounded_t = ct_ref[...].astype(bf16)
        out = sum(
            jnp.dot(piece, rounded_g, preferred_element_type=f32) for piece in split(lhs[...])
        )
        for m in range(mats):
            left = geno_of(m) - out[m * 40 : m * 40 + 40]
            vst[:40, m * 256 : m * 256 + 256] = left
            vst[40:, m * 256 : m * 256 + 256] = jnp.zeros((8, 256), f32)
            if m == own:
                squares_g = squares_g - jnp.sum(
                    coef_g * (geno0 + left), axis=0, keepdims=True
                )
        more = sum(
            jnp.dot(rounded_t[:, :48], piece, preferred_element_type=f32)
            for piece in split(vst[...])
        )
        for m in range(mats):
            at = mats * 40 + m * 32
            corr[m] = out[at : at + 32] + more[:, m * 256 : m * 256 + 256]
        mean_g = jnp.maximum(squares_g, 0.0) / samples
        sg_ref[...] = jnp.broadcast_to(lax.rsqrt(mean_g + epsilon), (8, 256))

    def owned(m):
        outs = []
        for h in range(2):
            z_copy(h, m).wait_recv()
            total = low[h, m, zh] + inz[h, m]
            cols = slice(h * 128, h * 128 + 128)
            outs.append((total - corr[m, :, cols]) * st_ref[...] * sg_ref[0:1, cols])
        return outs

    loads[0].wait()
    loads[1].wait()
    spread = jnp.where(lax.rem(iota((32, 128), 1), 32) == iota((32, 128), 0), 1.0, 0.0)
    spread = spread.astype(bf16)
    for b in range(4):
        at = slice(b * 256, b * 256 + 256)
        q[own, at, :256] = geno_ref[at, :].astype(f32).astype(bf16)
        q[own, at, 256:] = lax.dot_general(
            cov_ref[:, at], spread, (((0,), (0,)), ((), ())), preferred_element_type=f32
        ).astype(bf16)
    xt[:32] = cov_ref[...]
    xt[32:] = jnp.where(iota((16, rows), 0) == 0, 1.0, 0.0).astype(bf16)
    eye = jnp.where(iota((256, 256), 0) == iota((256, 256), 1), 1.0, 0.0).astype(bf16)

    loads[2].wait()
    permute(0)
    for b in range(4):
        loads[3 + b].wait()
        at = slice(b * 256, b * 256 + 256)
        yt[at, :] = across(eye, y_ref[:, at]).astype(bf16)

    lane = iota((32, 128), 1)
    held = {"best": jnp.zeros((32, 128), f32)}

    def finish(m):
        left, right = owned(m)
        if m == own:
            out_ref[:32, :128] = left
            out_ref[:32, 128:] = right
            out_ref[32:, 128:] = jnp.zeros((8, 128), f32)
            return
        peak = jnp.max(jnp.maximum(jnp.abs(left), jnp.abs(right)), axis=1, keepdims=True)
        held["best"] = jnp.where(lane == m, peak, held["best"])

    def exchange():
        pm[...] = held["best"]
        for d in range(1, 8):
            to_tile(pm, pmin.at[d - 1], 1, d).start()

    stages = {"2": stage2, "3": stage3, "4": stage4, "5": stage5, "d": direct, "e": stage5d}
    whole = {"P": permute, "C": compute, "1": stage1, "f": finish}
    single = {
        "aux": aux_parts,
        "A1": lambda: stage1(aux, (1,)),
        "A2": lambda: stage2(aux, (1,)),
        "A3": lambda: direct(aux, (1,)),
        "A4": aux_low,
        "A5": aux_total,
        "A6": aux_row,
        "inv": invert,
        "ct": trait_side,
        "corr": corrections,
        "g1": gram_start,
        "g2": lambda: gram_pass(1),
        "g3": lambda: gram_pass(2),
        "T": exchange,
        "B": lambda: pl.semaphore_wait(barrier, len(met) + 7),
    }
    for name in ORDER:
        if name in single:
            single[name]()
        elif name[0] in whole:
            whole[name[0]](int(name[1]))
        else:
            stages[name[0]](int(name[1]), (int(name[2]),))
    best = held["best"]

    for h in range(2):
        all_of(in1.at[h], send1.at[h], recv1.at[0, 0, 0]).wait_send()
        all_of(in2.at[h], send2.at[h], recv2.at[0, 0, 0]).wait_send()
        all_of(inz.at[h], sendz.at[h], recvz.at[0, 0]).wait_send()
        all_of(ind.at[h], sendd.at[h], recvd.at[0, 0]).wait_send()
    all_of(tt.at[pl.ds(0, 7)], sendx.at[0], recvx.at[0]).wait_send()
    all_of(agu.at[x, pl.ds(0, 3)], sendx.at[2], recvx.at[2]).wait_send()
    both_copy().wait_send()
    all_of(ain1, send1.at[2], recv1.at[0, 0, 0]).wait_send()
    all_of(aind, sendd.at[2], recvd.at[0, 0]).wait_send()
    for n in range(3):
        sent = gin.at[pl.ds(0, 3 if n < 2 else 1)]
        all_of(sent, sendx.at[5 + n], recvx.at[5 + n]).wait_send()
    all_of(agu.at[pl.ds(0, 3)], sendx.at[3], recvx.at[3]).wait_send()
    all_of(pmin, sendx.at[1], recvx.at[1]).wait()
    for d in range(7):
        best = jnp.maximum(best, pmin[d])
    best = jnp.concatenate([best, jnp.zeros((96, 128), f32)], axis=0)
    out_ref[32:, :128] = jnp.transpose(best)[:8]


def scan(traits, covariates, genotypes, shuffles, samples):
    perms = shuffles.shape[0]
    mats = perms + 1
    ringed = perms - 1
    rows = traits.shape[0]
    vmem = pl.BlockSpec(memory_space=pltpu.VMEM)
    dma = pltpu.SemaphoreType.DMA
    return pl.pallas_call(
        functools.partial(scan_kernel, samples=samples),
        out_shape=jax.ShapeDtypeStruct((40, 256), f32),
        in_specs=[pl.BlockSpec(memory_space=pl.ANY)] * 4,
        out_specs=vmem,
        scratch_shapes=[
            pltpu.VMEM(traits.shape, bf16),
            pltpu.VMEM(covariates.shape[::-1], bf16),
            pltpu.VMEM(genotypes.shape, jnp.int32),
            pltpu.VMEM(shuffles.shape, jnp.int32),
            dma((7,)),
            pltpu.VMEM((1024, rows), bf16),
            pltpu.VMEM((mats, rows, 384), bf16),
            pltpu.VMEM((48, rows), bf16),
            pltpu.VMEM((32, 32, 128), f32),
            pltpu.VMEM((2, mats, 4, 2, 4, 32, 128), f32),
            pltpu.VMEM((2, mats, 6, 4, 32, 128), f32),
            pltpu.VMEM((2, mats, 4, 2, 32, 128), f32),
            pltpu.VMEM((2, ringed, 6, 32, 128), f32),
            pltpu.VMEM((2, mats, 2, 32, 128), f32),
            pltpu.VMEM((2, mats, 32, 128), f32),
            pltpu.VMEM((2, mats - ringed, 3, 2, 32, 128), f32),
            pltpu.VMEM((4, 2, 4, 24, 128), f32),
            pltpu.VMEM((6, 4, 24, 128), f32),
            pltpu.VMEM((4, 2, 24, 128), f32),
            pltpu.VMEM((3, 2, 24, 128), f32),
            pltpu.VMEM((2, 24, 128), f32),
            pltpu.VMEM((2, 24, 128), f32),
            pltpu.VMEM((4, 4, 2, 16, 128), f32),
            pltpu.VMEM((8, 8, 128), f32),
            pltpu.VMEM((4, 40, 128), f32),
            pltpu.VMEM((7, 40, 128), f32),
            pltpu.VMEM((128, 128), f32),
            pltpu.VMEM((32, 128), f32),
            pltpu.VMEM((mats * 72, 128), f32),
            pltpu.VMEM((48, mats * 256), f32),
            pltpu.VMEM((mats, 32, 256), f32),
            pltpu.VMEM((32, 128), f32),
            pltpu.VMEM((8, 256), f32),
            pltpu.VMEM((32, 128), f32),
            pltpu.VMEM((7, 32, 128), f32),
            dma((3,)), dma((2, mats + 1, 3)),
            dma((2,)), dma((2, ringed, 3)),
            dma((2,)), dma((2, mats)),
            dma((3,)), dma((2, mats + 1 - ringed)),
            dma((8,)), dma((8,)),
        ],
        compiler_params=pltpu.CompilerParams(
            collective_id=0, has_side_effects=True, vmem_limit_bytes=56 * 1024 * 1024
        ),
    )(traits, covariates.T, genotypes, shuffles)


def shards(traits, covariates, genotypes, shuffles):
    samples = traits.shape[0] * lax.axis_size("samp")
    out = scan(traits, covariates, genotypes, shuffles, samples)
    return (out[:32], out[32 : 32 + shuffles.shape[0], :32])


def solution(mesh):
    placed = (P("samp", None), P("samp", None), P("samp", "tile"), P(None, "samp"))
    return jax.shard_map(
        shards,
        mesh=mesh,
        in_specs=placed,
        out_specs=(P("samp", "tile"), P(None, "samp")),
        check_vma=False,
    )
```

time: 75.4 us -> 72 us (0.955)
  Pallas kernels: 71.9 us -> 68.6 us
    pallas_call x1, Pallas kernels: 71.9 us -> 68.6 us  [scan(): pl.pallas_call(functools.partial(scan_kernel, samples=samples), out_shape...]
where the time goes in v5:
time: 72 us; the launch traced here: 71.8 us
  Pallas kernels  68.6 us (95%)
  local copies, waits for them, and re-layouts  2.64 us (4%)
    pallas_call x1, Pallas kernels, scan(): pl.pallas_call(functools.partial(scan_kernel, samples=samples), out_shape...  68.6 us
    slice x2, local copies, waits for them, and re-layouts, shards(): return (out[:32], out[32:32 + shuffles.shape[0], :32])  2.64 us

profile of v5, /device:TPU:1, one launch (start us, length us, event | category | flops | bytes accessed | tf_op | source)
XLA Modules:
  0.0 71.8 jit_solution(4398269150535721079)
XLA Ops:
  0.6 68.6 %shard_map.59 = f32[40,256]{1,0:T(8,128)} custom-call(bf16[1024,1024]{1,0:T(8,128)(2,1)} %y_hbm.1, bf16[32,1024]{1,0:T(8,128)(2,1)} %bitcast.1, s32[1024,256]{1,0:T(8,128)} %geno_hbm.1, s32[6,1024]{1,0:T(8,128)} %order_hbm.1), custom_call_target="tpu_custom_call" | custom-call | tf_op jit(solution)/shard_map/pallas_call | solution.py:519
  69.2 1.3 %slice.7 = f32[6,32]{1,0:T(8,128)} slice(f32[40,256]{1,0:T(8,128)} %shard_map.59), slice={[32:38], [0:32]} | slice | bytes 1536 | tf_op jit(solution)/shard_map/slice | solution.py:575
  70.5 1.4 %slice.6 = f32[32,256]{1,0:T(8,128)} slice(f32[40,256]{1,0:T(8,128)} %shard_map.59), slice={[0:32], [0:256]} | slice | bytes 65536 | tf_op jit(solution)/shard_map/slice | solution.py:575

commit v6 on v5

--- a/solution.py
+++ b/solution.py
@@ -18,14 +18,14 @@
 
 
 ORDER = (
-    "C0", "B", "10", "P1", "C1", "11", "P3", "g1", "P2", "200", "C3", "13",
-    "P5", "C2", "P4", "12", "aux", "A1", "210", "C5", "g2", "201", "220", "A2",
-    "221", "C4", "211", "15", "231", "A3", "250", "230", "310", "321", "311", "C6",
-    "A4", "14", "320", "301", "300", "g3", "331", "330", "410", "241", "421", "240",
-    "251", "411", "A5", "400", "401", "16", "inv", "341", "431", "430", "420", "d51",
-    "510", "260", "521", "340", "501", "441", "500", "d50", "261", "A6", "531", "530",
-    "511", "440", "520", "d60", "e51", "541", "ct", "e50", "d61", "540", "corr", "f1",
-    "f0", "f2", "e60", "e61", "f5", "f4", "f3", "T", "f6",
+    "C0", "B", "10", "g1", "P1", "C1", "11", "P2", "C2", "201", "P4", "12",
+    "P3", "C4", "14", "P5", "aux", "A1", "301", "200", "C3", "13", "210", "240",
+    "A2", "241", "401", "211", "221", "C5", "230", "A3", "15", "340", "341", "310",
+    "231", "311", "321", "C6", "A4", "220", "251", "g2", "16", "501", "441", "300",
+    "440", "331", "421", "250", "330", "411", "260", "A5", "320", "431", "261", "g3",
+    "d51", "521", "541", "540", "410", "400", "d50", "420", "511", "430", "A6", "531",
+    "d61", "510", "d60", "500", "e51", "520", "530", "e50", "inv", "ct", "e61", "e60",
+    "corr", "f4", "f2", "f1", "f0", "f3", "f5", "T", "f6",
 )
 
 
@@ -507,6 +507,11 @@
         best = jnp.maximum(best, pmin[d])
     best = jnp.concatenate([best, jnp.zeros((96, 128), f32)], axis=0)
     out_ref[32:, :128] = jnp.transpose(best)[:8]
+
+
+def hand_out(both_ref, obs_ref, peak_ref):
+    obs_ref[...] = both_ref[:32]
+    peak_ref[...] = both_ref[32 : 32 + peak_ref.shape[0], :32]
 
 
 def scan(traits, covariates, genotypes, shuffles, samples):
@@ -572,7 +577,14 @@
 def shards(traits, covariates, genotypes, shuffles):
     samples = traits.shape[0] * lax.axis_size("samp")
     out = scan(traits, covariates, genotypes, shuffles, samples)
-    return (out[:32], out[32 : 32 + shuffles.shape[0], :32])
+    perms = shuffles.shape[0]
+    return pl.pallas_call(
+        hand_out,
+        out_shape=(
+            jax.ShapeDtypeStruct((32, 256), f32),
+            jax.ShapeDtypeStruct((perms, 32), f32),
+        ),
+    )(out)
 
 
 def solution(mesh):

time: 72 us -> 69.1 us (0.960)
  local copies, waits for them, and re-layouts: 2.64 us -> 0 us
    slice x2 -> x0, local copies, waits for them, and re-layouts: 2.64 us -> none  [shards(): return (out[:32], out[32:32 + shuffles.shape[0], :32])]
    pallas_call x1, Pallas kernels: 68.6 us -> 66.9 us  [scan(): pl.pallas_call(functools.partial(scan_kernel, samples=samples), out_shape...]
    pallas_call x0 -> x1, Pallas kernels: none -> 1.4 us  [shards(): pl.pallas_call(hand_out, out_shape=(jax.ShapeDtypeStruct((32, 256), f32),...]
where the time goes in v6:
time: 69.1 us; the launch traced here: 68.9 us
  Pallas kernels  68.3 us (99%)
    pallas_call x1, Pallas kernels, scan(): pl.pallas_call(functools.partial(scan_kernel, samples=samples), out_shape...  66.9 us
    pallas_call x1, Pallas kernels, shards(): pl.pallas_call(hand_out, out_shape=(jax.ShapeDtypeStruct((32, 256), f32),...  1.4 us

profile of v6, /device:TPU:1, one launch (start us, length us, event | category | flops | bytes accessed | tf_op | source)
XLA Modules:
  0.0 68.9 jit_solution(7733245467183638215)
XLA Ops:
  0.6 66.9 %shard_map.59.both_ref = f32[40,256]{1,0:T(8,128)} custom-call(bf16[1024,1024]{1,0:T(8,128)(2,1)} %y_hbm.1, bf16[32,1024]{1,0:T(8,128)(2,1)} %bitcast.1, s32[1024,256]{1,0:T(8,128)} %geno_hbm.1, s32[6,1024]{1,0:T(8,128)} %order_hbm.1), custom_call_target="tpu_custom_call" | custom-call | tf_op jit(solution)/shard_map/pallas_call | solution.py:524
  67.5 1.4 %shard_map.60 = (f32[32,256]{1,0:T(8,128)}, f32[6,32]{1,0:T(8,128)}) custom-call(f32[40,256]{1,0:T(8,128)} %shard_map.59.both_ref), custom_call_target="tpu_custom_call" | custom-call | tf_op jit(solution)/shard_map/pallas_call | solution.py:581

commit v7 on v6

--- a/solution.py
+++ b/solution.py
@@ -418,7 +418,7 @@
             z_copy(h, m).wait_recv()
             total = low[h, m, zh] + inz[h, m]
             cols = slice(h * 128, h * 128 + 128)
-            outs.append((total - corr[m, :, cols]) * st_ref[...] * sg_ref[0:1, cols])
+            outs.append((total - corr[m, :, cols]) * sg_ref[0:1, cols])
         return outs
 
     loads[0].wait()
@@ -448,12 +448,12 @@
     def finish(m):
         left, right = owned(m)
         if m == own:
-            out_ref[:32, :128] = left
-            out_ref[:32, 128:] = right
+            out_ref[:32, :128] = left * st_ref[...]
+            out_ref[:32, 128:] = right * st_ref[...]
             out_ref[32:, 128:] = jnp.zeros((8, 128), f32)
             return
         peak = jnp.max(jnp.maximum(jnp.abs(left), jnp.abs(right)), axis=1, keepdims=True)
-        held["best"] = jnp.where(lane == m, peak, held["best"])
+        held["best"] = jnp.where(lane == m, peak * st_ref[...], held["best"])
 
     def exchange():
         pm[...] = held["best"]

time: 69.1 us -> 69.1 us (level)
  no operation moved by 1% of the time
where the time goes in v7:
time: 69.1 us; the launch traced here: 68.9 us
  Pallas kernels  68.3 us (99%)
    pallas_call x1, Pallas kernels, scan(): pl.pallas_call(functools.partial(scan_kernel, samples=samples), out_shape...  66.9 us
    pallas_call x1, Pallas kernels, shards(): pl.pallas_call(hand_out, out_shape=(jax.ShapeDtypeStruct((32, 256), f32),...  1.4 us

profile of v7, /device:TPU:1, one launch (start us, length us, event | category | flops | bytes accessed | tf_op | source)
XLA Modules:
  0.0 68.9 jit_solution(4631290711061021669)
XLA Ops:
  0.6 66.9 %shard_map.59.both_ref = f32[40,256]{1,0:T(8,128)} custom-call(bf16[1024,1024]{1,0:T(8,128)(2,1)} %y_hbm.1, bf16[32,1024]{1,0:T(8,128)(2,1)} %bitcast.1, s32[1024,256]{1,0:T(8,128)} %geno_hbm.1, s32[6,1024]{1,0:T(8,128)} %order_hbm.1), custom_call_target="tpu_custom_call" | custom-call | tf_op jit(solution)/shard_map/pallas_call | solution.py:524
  67.5 1.4 %shard_map.60 = (f32[32,256]{1,0:T(8,128)}, f32[6,32]{1,0:T(8,128)}) custom-call(f32[40,256]{1,0:T(8,128)} %shard_map.59.both_ref), custom_call_target="tpu_custom_call" | custom-call | tf_op jit(solution)/shard_map/pallas_call | solution.py:581
